TPU v7x, 32 devices: a whole 2x2x4 slice. The times are simulated.
32 devices in a mesh: graph: 16 (over z, y, core), chan: 2 (over x).
Axes of the slice: x: 2, y: 2, z: 4, core: 2. Of those that a mesh axis runs over, the one named last changes fastest.
Arguments:
- embed: bfloat16 [25, 512, 2048], P(None, 'chan', 'graph'), may hold values from -200 to 200
- gain: float32 [5, 512], P(None, 'chan'), may hold values from 0.25 to 1.75
- w_zero: bfloat16 [5, 512, 2560], P(None, 'chan'), may hold values from -0.125 to 0.125
- w_one: bfloat16 [2, 4, 512, 2048], P(None, None, 'chan'), may hold values from -0.125 to 0.125
- w_two: bfloat16 [2, 3, 512, 1536], P(None, None, 'chan'), may hold values from -0.15625 to 0.15625
- rot_table: float32 [19, 25, 256], replicated, may hold values from -1 to 1, as said below
- face_atoms: int32 [512], P('graph'), may hold values from 0 to 127, as said below
- edge_source: int32 [2048], P('graph'), may hold values from 0 to 159
- edge_target: int32 [2048], P('graph'), may hold values from 0 to 127
- rot_index: int32 [2048], P('graph'), may hold values from 0 to 255
- edge_weight: float32 [2048], P('graph'), may hold values from 0.2 to 1
- cotangent: bfloat16 [25, 512, 2048], P(None, 'chan', 'graph'), may hold values from -1.5 to 1.5
Outputs:
- update: bfloat16 [25, 512, 2048], P(None, 'chan', 'graph')
- grad_embed: bfloat16 [25, 512, 2048], P(None, 'chan', 'graph')
- grad_zero: float32 [5, 512, 2560], P(None, 'chan', 'graph')
- grad_one: float32 [2, 4, 512, 2048], P(None, None, 'chan', 'graph')
- grad_two: float32 [2, 3, 512, 1536], P(None, None, 'chan', 'graph')
Inputs may be any that keep to these rules, and one draw needn't show every extreme that they name: `rot_table`: for every rotation, frame row (m, l) is nonzero only on the 2l + 1 coefficients of degree l, where it is row l + m of an orthogonal (2l + 1)-square matrix shared by the rows of that degree; the degree-0 entry is 1. `face_atoms`: block b holds 32 distinct atom indices counted from the first atom of block b: the first 16 lie at the face toward block b - 1, the last 16 at the face toward block b + 1. `edge_source`: read as in the step that defines src. `edge_target`: counted from the first atom of the edge's block.
All inputs are finite; a program needn't handle non-finite values.
Results may differ from a plain program's by a relative error of at most 0.0062.
Values may be sent and summed in bfloat16 or wider, within the bound.
A program may use at most 192 MiB of HBM per device.

v0:
```python
import jax
import jax.numpy as jnp
from jax import lax
from jax.sharding import PartitionSpec as P

C = 512


EPSILON = 1e-06
HIGHEST = lax.Precision.HIGHEST
FRAME = (
    (0, 0),
    (1, 0),
    (2, 0),
    (3, 0),
    (4, 0),
    (1, 1),
    (2, 1),
    (3, 1),
    (4, 1),
    (1, -1),
    (2, -1),
    (3, -1),
    (4, -1),
    (2, 2),
    (3, 2),
    (4, 2),
    (2, -2),
    (3, -2),
    (4, -2),
)


def with_halo(block, sides, width):
    for axis, dim in sides:
        count = lax.axis_size(axis)
        forward = [(i, i + 1) for i in range(count - 1)]
        forward.append((count - 1, 0))
        backward = [(target, source) for source, target in forward]
        low = lax.ppermute(
            lax.slice_in_dim(block, block.shape[dim] - width, None, axis=dim), axis, forward
        )
        high = lax.ppermute(lax.slice_in_dim(block, 0, width, axis=dim), axis, backward)
        block = jnp.concatenate([low, block, high], axis=dim)
    return block


def gain_rows(gain):
    pieces = [
        jnp.broadcast_to(gain[degree : degree + 1], (2 * degree + 1, gain.shape[1]))
        for degree in range(5)
    ]
    return jnp.concatenate(pieces, axis=0)


def product(left, right):
    return jnp.dot(left, right, preferred_element_type=jnp.float32)


def across(left, right):
    return lax.dot_general(
        left, right, (((0,), (0,)), ((), ())), preferred_element_type=jnp.float32
    )


def outer(left, right):
    return lax.dot_general(
        left, right, (((1,), (1,)), ((), ())), preferred_element_type=jnp.float32
    )


def stack_frame(parts, width, edges):
    row_counts = (5, 4, 4, 3, 3)
    return jnp.concatenate(
        [part.reshape(rows, width, edges) for part, rows in zip(parts, row_counts)], axis=0
    )


def rotate_in(values, rotations):
    rows = []
    for row, pair in enumerate(FRAME):
        first = pair[0] * pair[0]
        total = rotations[row, first][None, :] * values[first].astype(jnp.float32)
        for column in range(first + 1, first + 2 * pair[0] + 1):
            total = total + rotations[row, column][None, :] * values[column].astype(jnp.float32)
        rows.append(total)
    return jnp.stack(rows)


def rotate_out(values, rotations):
    columns = []
    for degree in range(5):
        members = [row for row, pair in enumerate(FRAME) if pair[0] == degree]
        for column in range(degree * degree, (degree + 1) * (degree + 1)):
            total = rotations[members[0], column][None, :] * values[members[0]]
            for row in members[1:]:
                total = total + rotations[row, column][None, :] * values[row]
            columns.append(total)
    return jnp.stack(columns)


def mix_part(w_zero, w_one, w_two, piece):
    count = piece.shape[1]
    edges = piece.shape[2]
    outputs = w_zero.shape[1]

    def columns(weight, blocks):
        shaped = weight.reshape(blocks * outputs, blocks, weight.shape[-1] // blocks)
        return shaped.reshape(blocks * outputs, blocks * count)

    def frame_rows(first, blocks):
        return piece[first : first + blocks].reshape(blocks * count, edges)

    parts = [product(columns(w_zero, 5), frame_rows(0, 5))]
    for weights, first, blocks in ((w_one, 5, 4), (w_two, 13, 3)):
        real_part = columns(weights[0], blocks)
        imag_part = columns(weights[1], blocks)
        plus = frame_rows(first, blocks)
        minus = frame_rows(first + blocks, blocks)
        parts.append(product(real_part, plus) - product(imag_part, minus))
        parts.append(product(real_part, minus) + product(imag_part, plus))
    return tuple(parts)


def mix_backward(w_zero, w_one, w_two, grads, frame):
    outputs = grads.shape[1]
    width = frame.shape[1]
    edges = grads.shape[2]

    def grad_rows(first, blocks):
        return grads[first : first + blocks].reshape(blocks * outputs, edges)

    def frame_rows(first, blocks):
        return frame[first : first + blocks].reshape(blocks * width, edges)

    zero_weight = w_zero.reshape(5 * outputs, 5 * width)
    grad_first = grad_rows(0, 5)
    back = [across(zero_weight, grad_first)]
    weight_zero = outer(grad_first, frame_rows(0, 5)).reshape(5, outputs, 5 * width)
    pairs = []
    for weights, first, blocks in ((w_one, 5, 4), (w_two, 13, 3)):
        real_part = weights[0].reshape(blocks * outputs, blocks * width)
        imag_part = weights[1].reshape(blocks * outputs, blocks * width)
        grad_plus = grad_rows(first, blocks)
        grad_minus = grad_rows(first + blocks, blocks)
        frame_plus = frame_rows(first, blocks)
        frame_minus = frame_rows(first + blocks, blocks)
        back.append(across(real_part, grad_plus) + across(imag_part, grad_minus))
        back.append(across(real_part, grad_minus) - across(imag_part, grad_plus))
        real_grad = outer(grad_plus, frame_plus) + outer(grad_minus, frame_minus)
        imag_grad = outer(grad_minus, frame_plus) - outer(grad_plus, frame_minus)
        pairs.append(
            jnp.stack(
                [
                    real_grad.reshape(blocks, outputs, blocks * width),
                    imag_grad.reshape(blocks, outputs, blocks * width),
                ]
            )
        )
    return (stack_frame(back, width, edges), weight_zero, pairs[0], pairs[1])


def shards(
    embed,
    gain,
    w_zero,
    w_one,
    w_two,
    rot_table,
    face_atoms,
    edge_source,
    edge_target,
    rot_index,
    edge_weight,
    cotangent,
):
    atoms = embed.shape[2]
    local = embed.shape[1]
    halo = face_atoms.shape[0] // 2
    edges = edge_source.shape[0]
    values = embed.astype(jnp.float32)
    gains = gain_rows(gain)
    squares = lax.psum(jnp.sum(values * values, axis=(0, 1)), "chan")
    inverse = lax.rsqrt(squares / (25 * C) + EPSILON)
    normed = (values * inverse[None, None, :] * gains[:, :, None]).astype(jnp.bfloat16)
    faces = jnp.take(normed, face_atoms, axis=2)
    beside_all = with_halo(faces, (("graph", 2),), halo)
    table = jnp.concatenate([normed, beside_all[:, :, :halo], beside_all[:, :, 3 * halo :]], axis=2)
    rotations = jnp.take(rot_table, rot_index, axis=2)
    own = rotate_in(jnp.take(table, edge_source, axis=2), rotations).astype(jnp.bfloat16)
    piece = lax.all_gather(own, "chan", axis=1, tiled=True)
    fresh = mix_part(w_zero, w_one, w_two, piece)
    totals = tuple((extra for extra in fresh))
    mixed = stack_frame(totals, local, edges)
    message = rotate_out(mixed * edge_weight[None, None, :], rotations).astype(jnp.bfloat16)
    landing = (edge_target[:, None] == jnp.arange(atoms, dtype=jnp.int32)[None, :]).astype(
        jnp.bfloat16
    )
    update = (
        product(message.reshape(25 * local, edges), landing)
        .reshape(25, local, atoms)
        .astype(jnp.bfloat16)
    )
    arriving = jnp.take(cotangent, edge_target, axis=2)
    grads = (rotate_in(arriving, rotations) * edge_weight[None, None, :]).astype(jnp.bfloat16)
    back, part_zero, part_one, part_two = mix_backward(w_zero, w_one, w_two, grads, piece)
    grad_zero, grad_one, grad_two = (
        lax.psum_scatter(part_zero, "graph", scatter_dimension=2, tiled=True),
        lax.psum_scatter(part_one, "graph", scatter_dimension=3, tiled=True),
        lax.psum_scatter(part_two, "graph", scatter_dimension=3, tiled=True),
    )
    spread = rotate_out(back, rotations)
    leaving = (
        edge_source[:, None] == jnp.arange(atoms + 2 * halo, dtype=jnp.int32)[None, :]
    ).astype(jnp.float32)
    collected = jnp.dot(
        spread.reshape(25 * C, edges),
        leaving,
        precision=HIGHEST,
        preferred_element_type=jnp.float32,
    ).reshape(25, C, atoms + 2 * halo)
    mine = lax.psum_scatter(collected, "chan", scatter_dimension=1, tiled=True)
    returned = with_halo(mine[:, :, atoms:], (("graph", 2),), halo)
    incoming = jnp.concatenate([returned[:, :, :halo], returned[:, :, 3 * halo :]], axis=2)
    owners = (face_atoms[:, None] == jnp.arange(atoms, dtype=jnp.int32)[None, :]).astype(
        jnp.float32
    )
    settled = jnp.dot(
        incoming.reshape(25 * local, 2 * halo),
        owners,
        precision=HIGHEST,
        preferred_element_type=jnp.float32,
    )
    grad_normed = mine[:, :, :atoms] + settled.reshape(25, local, atoms)
    tally = lax.psum(jnp.sum(values * gains[:, :, None] * grad_normed, axis=(0, 1)), "chan")
    grad_embed = (
        inverse[None, None, :] * gains[:, :, None] * grad_normed
        - values * (inverse**3 * tally / (25 * C))[None, None, :]
    ).astype(jnp.bfloat16)
    return (update, grad_embed, grad_zero, grad_one, grad_two)


def solution(mesh):
    placed = (
        P(None, "chan", "graph"),
        P(None, "chan"),
        P(None, "chan", None),
        P(None, None, "chan", None),
        P(None, None, "chan", None),
        P(),
        P("graph"),
        P("graph"),
        P("graph"),
        P("graph"),
        P("graph"),
        P(None, "chan", "graph"),
    )
    return jax.shard_map(
        shards,
        mesh=mesh,
        in_specs=placed,
        out_specs=(
            P(None, "chan", "graph"),
            P(None, "chan", "graph"),
            P(None, "chan", "graph"),
            P(None, None, "chan", "graph"),
            P(None, None, "chan", "graph"),
        ),
        check_vma=False,
    )
```

profile of v0, /device:TPU:0, one launch (start us, length us, event | category | flops | bytes accessed | tf_op | source)
XLA Modules:
  0.0 822.7 jit_solution(10396393119562080566)
XLA Ops:
  9.9 2.1 copy.48
  16.6 10.2 %slice_reduce_fusion.98 = (f32[128]{0:T(128)S(1)}, f32[128]{0:T(128)S(1)}, f32[128]{0:T(128)S(1)}, f32[128]{0:T(128)S(1)}, f32[128]{0:T(128)S(1)}, /*index=5*/f3...) fusion(f32[19,25,128]{1,0,2:T(8,128)S(1)} %select_bitcast_fusion.2), kind=kLoop, calls=%fused_computation.713 | loop fusion | bytes 19456 | tf_op jit(solution)/shard_map/slice | solution.py:83
  26.8 10.6 %slice_reduce_fusion.81 = (f32[128]{0:T(128)S(1)}, f32[128]{0:T(128)S(1)}, f32[128]{0:T(128)S(1)}, f32[128]{0:T(128)S(1)}, f32[128]{0:T(128)S(1)}, /*index=5*/f3...) fusion(f32[19,25,128]{1,0,2:T(8,128)S(1)} %select_bitcast_fusion.2), kind=kLoop, calls=%fused_computation.696 | loop fusion | bytes 19456 | tf_op jit(solution)/shard_map/slice | solution.py:83
  37.4 10.0 %slice_reduce_fusion.57 = (f32[128]{0:T(128)}, f32[128]{0:T(128)}, f32[128]{0:T(128)}, f32[128]{0:T(128)}, f32[128]{0:T(128)}, /*index=5*/f32[128]{0:T(128)}, f3...) fusion(f32[19,25,128]{1,0,2:T(8,128)S(1)} %select_bitcast_fusion.2), kind=kLoop, calls=%fused_computation.672 | loop fusion | bytes 19456 | tf_op jit(solution)/shard_map/slice | solution.py:83
  47.4 10.4 %slice_reduce_fusion.41 = (f32[128]{0:T(128)}, f32[128]{0:T(128)}, f32[128]{0:T(128)}, f32[128]{0:T(128)}, f32[128]{0:T(128)S(1)}, /*index=5*/f32[128]{0:T(128)S...) fusion(f32[19,25,128]{1,0,2:T(8,128)S(1)} %select_bitcast_fusion.2), kind=kLoop, calls=%fused_computation.656 | loop fusion | bytes 19456 | tf_op jit(solution)/shard_map/slice | solution.py:83
  57.9 10.5 %slice_reduce_fusion.20 = (f32[128]{0:T(128)}, f32[128]{0:T(128)}, f32[128]{0:T(128)S(1)}, f32[128]{0:T(128)S(1)}, f32[128]{0:T(128)S(1)}, /*index=5*/f32[128]{0...) fusion(f32[19,25,128]{1,0,2:T(8,128)S(1)} %select_bitcast_fusion.2), kind=kLoop, calls=%fused_computation.635 | loop fusion | bytes 19456 | tf_op jit(solution)/shard_map/slice | solution.py:83
  68.4 10.3 %slice_reduce_fusion.8 = (f32[128]{0:T(128)}, f32[128]{0:T(128)S(1)}, f32[128]{0:T(128)S(1)}, f32[128]{0:T(128)S(1)}, f32[128]{0:T(128)S(1)}, /*index=5*/f32[128...) fusion(f32[19,25,128]{1,0,2:T(8,128)S(1)} %select_bitcast_fusion.2), kind=kLoop, calls=%fused_computation.623 | loop fusion | bytes 19456 | tf_op jit(solution)/shard_map/slice | solution.py:83
  78.7 3.4 copy.59
  82.0 2.0 gather_fusion.3
  84.0 4.2 copy.60
  126.1 6.2 fusion.233
  132.3 3.7 copy.49
  136.2 96.1 %reduce-scatter.5.cloned.1.call-done = f32[25,256,160]{1,2,0:T(8,128)} async-done(((f32[25,512,160]{1,2,0:T(8,128)}), f32[25,256,160]{1,2,0:T(8,128)}) %reduce-scatter.5.cloned.1.call-update) | async-done | bytes 4096016 | tf_op jit(solution)/shard_map/reduce_scatter | solution.py:222
  233.6 3.6 collective-permute-start.3
  239.0 3.7 collective-permute-done.3
  242.7 4.6 collective-permute-done.2
  247.3 6.0 fusion.4
  253.3 4.9 all-reduce
  258.2 4.6 fusion.6
  264.0 2.3 copy.50
  266.3 2.3 gather_fusion.1
  270.9 2.1 collective-permute-done.1
  273.0 4.7 collective-permute-done
  277.9 2.7 copy.52
  280.6 3.9 gather_fusion.2
  284.5 4.3 copy.53
  311.8 35.2 %all-gather.2.cloned.1.call-done = bf16[19,512,128]{2,1,0:T(8,128)(2,1)} async-done(((bf16[19,256,128]{2,1,0:T(8,128)(2,1)}), bf16[19,512,128]{2,1,0:T(8,128)(2,1)}) %all-gather.2.cloned.1.call-update) | async-done | bytes 2490384 | tf_op jit(solution)/shard_map/all_gather | solution.py:191
  349.0 2.9 fusion.264
  351.9 2.9 convolution_subtract_fusion.1
  354.8 6.1 copy.65
  360.9 5.3 convolution_add_fusion.1
  366.2 6.0 copy.64
  372.2 8.7 %pad_maximum_fusion.1 = f32[2,3,256,1536]{2,3,1,0:T(8,128)} fusion(f32[1,3,256,1536]{2,3,1,0:T(8,128)} %copy.65, f32[1,3,256,1536]{2,3,1,0:T(8,128)} %copy.64), kind=kLoop, calls=%fused_computation.5 | loop fusion | flops 2359296 | bytes 18874368 | tf_op jit(solution)/shard_map/stack | solution.py:153
  382.9 8.6 %fusion.266 = f32[5,256,2560]{1,2,0:T(8,128)} fusion(bf16[19,256,128]{2,1,0:T(8,128)(2,1)} %copy-done.18, bf16[2560,128,1]{1,0,2:T(8,128)(2,1)S(1)} %bitcast.227), kind=kOutput, calls=%fused_computation.775 | convolution fusion | flops 838860800 | bytes 15007744 | tf_op jit(solution)/shard_map/dot_general | solution.py:67
  393.0 2.3 fusion.263
  399.0 6.9 pad_maximum_fusion
  406.0 3.7 copy.66
  409.7 6.2 convolution_bitcast_fusion.1
  415.8 2.2 copy.54
  418.0 3.8 fusion.254
  421.9 2.3 fusion.11
  424.2 2.1 copy.70
  426.3 3.9 fusion.255
  430.2 2.3 fusion.12
  432.5 2.1 copy.71
  459.9 32.3 %reduce-scatter.11.cloned.1.call-done = f32[2,3,256,96]{2,3,1,0:T(8,128)} async-done(((f32[2,3,256,1536]{2,3,1,0:T(8,128)}), f32[2,3,256,96]{2,3,1,0:T(8,128)}) %reduce-scatter.11.cloned.1.call-update) | async-done | bytes 589840 | tf_op jit(solution)/shard_map/reduce_scatter | solution.py:210
  492.2 142.6 %reduce-scatter.7.cloned.1.call-done = f32[5,256,160]{1,2,0:T(8,128)} async-done(((f32[5,256,2560]{1,2,0:T(8,128)}), f32[5,256,160]{1,2,0:T(8,128)}) %reduce-scatter.7.cloned.1.call-update) | async-done | bytes 819216 | tf_op jit(solution)/shard_map/reduce_scatter | solution.py:208
  634.8 180.9 %reduce-scatter.9.cloned.1.call-done = f32[2,4,256,128]{3,2,1,0:T(8,128)} async-done(((f32[2,4,256,2048]{3,2,1,0:T(8,128)}), f32[2,4,256,128]{3,2,1,0:T(8,128)}) %reduce-scatter.9.cloned.1.call-update) | async-done | bytes 1048592 | tf_op jit(solution)/shard_map/reduce_scatter | solution.py:209
  (377 shorter events, 108.2 us)
Async XLA Ops:
  7.2 225.2 %reduce-scatter.5.cloned.1.call-start = ((), (), s32[]{:S(2)}) async-start(), calls=%async_computation.5 | async-start | bytes 12288000 | tf_op jit(solution)/shard_map/reduce_scatter | solution.py:222
  26.8 81.5 %copy-start.91 = (f32[128]{0:T(128)}, f32[128]{0:T(128)S(1)}, u32[]{:S(2)}) copy-start(f32[128]{0:T(128)S(1)} %get-tuple-element.134) | copy-start | bytes 1540
  26.8 264.2 %copy-start.86 = (f32[128]{0:T(128)}, f32[128]{0:T(128)S(1)}, u32[]{:S(2)}) copy-start(f32[128]{0:T(128)S(1)} %get-tuple-element.133) | copy-start | bytes 1540
  26.8 265.5 %copy-start.38 = (f32[128]{0:T(128)}, f32[128]{0:T(128)S(1)}, u32[]{:S(2)}) copy-start(f32[128]{0:T(128)S(1)} %get-tuple-element.128) | copy-start | bytes 1540
  26.8 265.5 %copy-start.48 = (f32[128]{0:T(128)}, f32[128]{0:T(128)S(1)}, u32[]{:S(2)}) copy-start(f32[128]{0:T(128)S(1)} %get-tuple-element.129) | copy-start | bytes 1540
  26.8 265.5 %copy-start.58 = (f32[128]{0:T(128)}, f32[128]{0:T(128)S(1)}, u32[]{:S(2)}) copy-start(f32[128]{0:T(128)S(1)} %get-tuple-element.130) | copy-start | bytes 1540
  26.8 265.5 %copy-start.68 = (f32[128]{0:T(128)}, f32[128]{0:T(128)S(1)}, u32[]{:S(2)}) copy-start(f32[128]{0:T(128)S(1)} %get-tuple-element.131) | copy-start | bytes 1540
  26.8 265.5 %copy-start.78 = (f32[128]{0:T(128)}, f32[128]{0:T(128)S(1)}, u32[]{:S(2)}) copy-start(f32[128]{0:T(128)S(1)} %get-tuple-element.132) | copy-start | bytes 1540
  26.8 266.2 %copy-start.28 = (f32[128]{0:T(128)}, f32[128]{0:T(128)S(1)}, u32[]{:S(2)}) copy-start(f32[128]{0:T(128)S(1)} %get-tuple-element.127) | copy-start | bytes 1540
  37.4 258.5 %copy-start.72 = (f32[128]{0:T(128)}, f32[128]{0:T(128)S(1)}, u32[]{:S(2)}) copy-start(f32[128]{0:T(128)S(1)} %get-tuple-element.104) | copy-start | bytes 1540
  37.4 258.5 %copy-start.82 = (f32[128]{0:T(128)}, f32[128]{0:T(128)S(1)}, u32[]{:S(2)}) copy-start(f32[128]{0:T(128)S(1)} %get-tuple-element.105) | copy-start | bytes 1540
  37.4 259.9 %copy-start.32 = (f32[128]{0:T(128)}, f32[128]{0:T(128)S(1)}, u32[]{:S(2)}) copy-start(f32[128]{0:T(128)S(1)} %get-tuple-element.101) | copy-start | bytes 1540
  37.4 259.9 %copy-start.42 = (f32[128]{0:T(128)}, f32[128]{0:T(128)S(1)}, u32[]{:S(2)}) copy-start(f32[128]{0:T(128)S(1)} %get-tuple-element.102) | copy-start | bytes 1540
  37.4 259.9 %copy-start.52 = (f32[128]{0:T(128)}, f32[128]{0:T(128)S(1)}, u32[]{:S(2)}) copy-start(f32[128]{0:T(128)S(1)} %get-tuple-element.103) | copy-start | bytes 1540
  37.4 259.9 %copy-start.62 = (f32[128]{0:T(128)}, f32[128]{0:T(128)S(1)}, u32[]{:S(2)}) copy-start(f32[128]{0:T(128)S(1)} %get-tuple-element.98) | copy-start | bytes 1540
  47.4 249.9 %copy-start.24 = (f32[128]{0:T(128)}, f32[128]{0:T(128)S(1)}, u32[]{:S(2)}) copy-start(f32[128]{0:T(128)S(1)} %get-tuple-element.97) | copy-start | bytes 1540
  57.8 61.3 %copy-start.88 = (f32[128]{0:T(128)}, f32[128]{0:T(128)S(1)}, u32[]{:S(2)}) copy-start(f32[128]{0:T(128)S(1)} %get-tuple-element.76) | copy-start | bytes 1540
  57.8 243.7 %copy-start.56 = (f32[128]{0:T(128)}, f32[128]{0:T(128)S(1)}, u32[]{:S(2)}) copy-start(f32[128]{0:T(128)S(1)} %get-tuple-element.73) | copy-start | bytes 1540
  57.8 243.7 %copy-start.66 = (f32[128]{0:T(128)}, f32[128]{0:T(128)S(1)}, u32[]{:S(2)}) copy-start(f32[128]{0:T(128)S(1)} %get-tuple-element.74) | copy-start | bytes 1540
  57.8 243.7 %copy-start.76 = (f32[128]{0:T(128)}, f32[128]{0:T(128)S(1)}, u32[]{:S(2)}) copy-start(f32[128]{0:T(128)S(1)} %get-tuple-element.75) | copy-start | bytes 1540
  57.8 245.1 %copy-start.26 = (f32[128]{0:T(128)}, f32[128]{0:T(128)S(1)}, u32[]{:S(2)}) copy-start(f32[128]{0:T(128)S(1)} %get-tuple-element.70) | copy-start | bytes 1540
  57.9 245.1 %copy-start.36 = (f32[128]{0:T(128)}, f32[128]{0:T(128)S(1)}, u32[]{:S(2)}) copy-start(f32[128]{0:T(128)S(1)} %get-tuple-element.71) | copy-start | bytes 1540
  57.9 245.1 %copy-start.46 = (f32[128]{0:T(128)}, f32[128]{0:T(128)S(1)}, u32[]{:S(2)}) copy-start(f32[128]{0:T(128)S(1)} %get-tuple-element.72) | copy-start | bytes 1540
  68.4 238.1 %copy-start.30 = (f32[128]{0:T(128)}, f32[128]{0:T(128)S(1)}, u32[]{:S(2)}) copy-start(f32[128]{0:T(128)S(1)} %get-tuple-element.46) | copy-start | bytes 1540
  68.4 238.1 %copy-start.40 = (f32[128]{0:T(128)}, f32[128]{0:T(128)S(1)}, u32[]{:S(2)}) copy-start(f32[128]{0:T(128)S(1)} %get-tuple-element.47) | copy-start | bytes 1540
  68.4 238.1 %copy-start.50 = (f32[128]{0:T(128)}, f32[128]{0:T(128)S(1)}, u32[]{:S(2)}) copy-start(f32[128]{0:T(128)S(1)} %get-tuple-element.48) | copy-start | bytes 1540
  68.4 238.1 %copy-start.60 = (f32[128]{0:T(128)}, f32[128]{0:T(128)S(1)}, u32[]{:S(2)}) copy-start(f32[128]{0:T(128)S(1)} %get-tuple-element.49) | copy-start | bytes 1540
  68.4 238.1 %copy-start.70 = (f32[128]{0:T(128)}, f32[128]{0:T(128)S(1)}, u32[]{:S(2)}) copy-start(f32[128]{0:T(128)S(1)} %get-tuple-element.50) | copy-start | bytes 1540
  68.4 238.2 %copy-start.80 = (f32[128]{0:T(128)}, f32[128]{0:T(128)S(1)}, u32[]{:S(2)}) copy-start(f32[128]{0:T(128)S(1)} %get-tuple-element.51) | copy-start | bytes 1540
  78.6 231.5 %copy-start.34 = (f32[128]{0:T(128)}, f32[128]{0:T(128)S(1)}, u32[]{:S(2)}) copy-start(f32[128]{0:T(128)S(1)} %get-tuple-element.23) | copy-start | bytes 1540
  78.6 231.5 %copy-start.44 = (f32[128]{0:T(128)}, f32[128]{0:T(128)S(1)}, u32[]{:S(2)}) copy-start(f32[128]{0:T(128)S(1)} %get-tuple-element.24) | copy-start | bytes 1540
  78.7 231.5 %copy-start.54 = (f32[128]{0:T(128)}, f32[128]{0:T(128)S(1)}, u32[]{:S(2)}) copy-start(f32[128]{0:T(128)S(1)} %get-tuple-element.25) | copy-start | bytes 1540
  78.7 231.5 %copy-start.64 = (f32[128]{0:T(128)}, f32[128]{0:T(128)S(1)}, u32[]{:S(2)}) copy-start(f32[128]{0:T(128)S(1)} %get-tuple-element.26) | copy-start | bytes 1540
  78.7 231.5 %copy-start.74 = (f32[128]{0:T(128)}, f32[128]{0:T(128)S(1)}, u32[]{:S(2)}) copy-start(f32[128]{0:T(128)S(1)} %get-tuple-element.27) | copy-start | bytes 1540
  78.7 231.5 %copy-start.84 = (f32[128]{0:T(128)}, f32[128]{0:T(128)S(1)}, u32[]{:S(2)}) copy-start(f32[128]{0:T(128)S(1)} %get-tuple-element.28) | copy-start | bytes 1540
  89.1 9.2 %slice-start = ((s8[6553600]{0:T(1024)(128)(4,1)}), s8[4194304]{0:T(1024)(128)(4,1)S(1)}, s32[]{:S(2)}) async-start(s8[6553600]{0:T(1024)(128)(4,1)} %bitcast.197), calls=%async_computation.9 | async-start | bytes 8388608
  132.3 214.7 %all-gather.2.cloned.1.call-start = ((), (), s32[]{:S(2)}) async-start(), calls=%async_computation.4 | async-start | bytes 3735552 | tf_op jit(solution)/shard_map/all_gather | solution.py:191
  232.3 15.0 %copy-start.7 = (bf16[25,256,128]{1,2,0:T(8,128)(2,1)S(1)}, bf16[25,256,128]{1,2,0:T(8,128)(2,1)}, u32[]{:S(2)}) copy-start(bf16[25,256,128]{1,2,0:T(8,128)(2,1)} %copy.49) | copy-start | bytes 4915204
  233.6 9.0 %collective-permute-start.3 = (f32[25,256,16]{1,2,0:T(8,128)S(1)}, f32[25,256,16]{1,2,0:T(8,128)S(1)}, u32[]{:S(2)}, u32[]{:S(2)}) collective-permute-start(f32[25,256,16]{1,2,0:T(8,128)S(1)} %get-tuple-element.143), channel_id=1, source_target_pairs={{2,0},{4,2},{6,4},{8,6},{10,8},{12,10},{14,12},{16,14},{18,16},{20... | collective-permute-start | bytes 1228808 | tf_op jit(solution)/shard_map/ppermute | solution.py:43
  237.2 10.1 %collective-permute-start.2 = (f32[25,256,16]{1,2,0:T(8,128)S(1)}, f32[25,256,16]{1,2,0:T(8,128)S(1)}, u32[]{:S(2)}, u32[]{:S(2)}) collective-permute-start(f32[25,256,16]{1,2,0:T(8,128)S(1)} %get-tuple-element.142), channel_id=1, source_target_pairs={{0,2},{2,4},{4,6},{6,8},{8,10},{10,12},{12,14},{14,16},{16,18},{18... | collective-permute-start | bytes 1228808 | tf_op jit(solution)/shard_map/ppermute | solution.py:40
  268.6 9.1 %copy-start.9 = (bf16[25,256,128]{1,2,0:T(8,128)(2,1)S(1)}, bf16[25,256,128]{1,2,0:T(8,128)(2,1)}, u32[]{:S(2)}) copy-start(bf16[25,256,128]{1,2,0:T(8,128)(2,1)} %copy-done.8) | copy-start | bytes 4915204
  269.7 3.3 collective-permute-start.1
  269.7 7.9 collective-permute-start
  290.4 11.1 %copy-start.89 = (f32[128]{0:T(128)S(1)}, f32[128]{0:T(128)}, u32[]{:S(2)}) copy-start(f32[128]{0:T(128)} %copy-done.88) | copy-start | bytes 1540
  311.6 180.6 %reduce-scatter.11.cloned.1.call-start = ((), (), s32[]{:S(2)}) async-start(), calls=%async_computation.8 | async-start | bytes 10027008 | tf_op jit(solution)/shard_map/reduce_scatter | solution.py:210
  348.2 12.7 %copy-start.10 = (bf16[3,512,128]{2,1,0:T(8,128)(2,1)}, bf16[3,512,128]{2,1,0:T(8,128)(2,1)S(1)}, u32[]{:S(2)}) copy-start(bf16[3,512,128]{2,1,0:T(8,128)(2,1)S(1)} %get-tuple-element.144) | copy-start | bytes 1179652
  380.9 253.9 %reduce-scatter.7.cloned.1.call-start = ((), (), s32[]{:S(2)}) async-start(), calls=%async_computation.6 | async-start | bytes 13926400 | tf_op jit(solution)/shard_map/reduce_scatter | solution.py:208
  391.5 424.2 %reduce-scatter.9.cloned.1.call-start = ((), (), s32[]{:S(2)}) async-start(), calls=%async_computation.7 | async-start | bytes 17825792 | tf_op jit(solution)/shard_map/reduce_scatter | solution.py:209
  (67 other events, 241.8 us)
Sparse Core Ops, SparseCore 0:
  132.4 99.9 reduce-scatter.4
  311.7 35.2 all-gather.1
  381.0 111.1 reduce-scatter.10
  496.7 138.0 reduce-scatter.6
  639.3 176.3 reduce-scatter.8
where the time goes:
time: 833 us; the launch traced here: 823 us
  waiting for transfers between devices  502 us (60%)
  local copies, waits for them, and re-layouts  136 us (16%)
  other arithmetic  89.9 us (11%)
  matrix products  69.4 us (8%)
  between operations  16 us (2%)
    reduce_scatter x1, waiting for transfers between devices, shards(): lax.psum_scatter(part_one, 'graph', scatter_dimension=3, tiled=True)  181 us
    reduce_scatter x1, waiting for transfers between devices, shards(): lax.psum_scatter(part_zero, 'graph', scatter_dimension=2, tiled=True)  143 us
    reduce_scatter x1, waiting for transfers between devices, shards(): mine = lax.psum_scatter(collected, 'chan', scatter_dimension=1, tiled=True)  96.1 us
    slice x6, local copies, waits for them, and re-layouts, rotate_in(): total = rotations[row, first][None, :] * values[first].astype(jnp.float32)  61.9 us
    unnamed x87, other arithmetic  57.1 us
    all_gather x1, waiting for transfers between devices, shards(): piece = lax.all_gather(own, 'chan', axis=1, tiled=True)  35.2 us
    reduce_scatter x1, waiting for transfers between devices, shards(): lax.psum_scatter(part_two, 'graph', scatter_dimension=3, tiled=True)  32.3 us
    dot_general x9, matrix products, outer(): lax.dot_general(left, right, (((1,), (1,)), ((), ())), preferred_element_...  26.5 us
  transfers between devices with their start and end apart: 9, of which 9 were waited for; matrix products, arithmetic and copies ran while one was open for 10% of the time, Pallas kernels for 0%

commit v1 on v0

v1 whole, which is shorter than its diff:
```python
import functools

import jax
import jax.numpy as jnp
from jax import lax
from jax.experimental import pallas as pl
from jax.experimental.pallas import tpu as pltpu
from jax.sharding import PartitionSpec as P


EPSILON = 1e-06
HIGHEST = lax.Precision.HIGHEST
FRAME = (
    (0, 0),
    (1, 0),
    (2, 0),
    (3, 0),
    (4, 0),
    (1, 1),
    (2, 1),
    (3, 1),
    (4, 1),
    (1, -1),
    (2, -1),
    (3, -1),
    (4, -1),
    (2, 2),
    (3, 2),
    (4, 2),
    (2, -2),
    (3, -2),
    (4, -2),
)


def gain_rows(gain):
    pieces = [
        jnp.broadcast_to(gain[degree : degree + 1], (2 * degree + 1, gain.shape[1]))
        for degree in range(5)
    ]
    return jnp.concatenate(pieces, axis=0)


def product(left, right):
    return jnp.dot(left, right, preferred_element_type=jnp.float32)


def across(left, right):
    return lax.dot_general(
        left, right, (((0,), (0,)), ((), ())), preferred_element_type=jnp.float32
    )


def contract(left, right):
    return lax.dot_general(left, right, (((2,), (1,)), ((), ())), preferred_element_type=jnp.float32)


def frames_kernel(*refs):
    pairs, (rotations, scale, out) = refs[:-3], refs[-3:]
    count, width = pairs[0].shape[0], pairs[0].shape[1]
    total = None
    for values, picks in zip(pairs[0::2], pairs[1::2]):
        part = product(values[...].reshape(count * width, values.shape[2]), picks[...])
        total = part if total is None else total + part
    total = total.reshape(count, width, total.shape[1])
    for row, (degree, _) in enumerate(FRAME):
        first = degree * degree
        entry = row * count + first
        line = rotations[entry : entry + 1, :] * total[first]
        for step in range(1, 2 * degree + 1):
            entry = row * count + first + step
            line = line + rotations[entry : entry + 1, :] * total[first + step]
        out[row] = (line * scale[...]).astype(out.dtype)


def to_frames(pairs, rotations, scale):
    count, local = pairs[0][0].shape[0], pairs[0][0].shape[1]
    edges = scale.shape[1]
    block = min(64, local)
    operands, specs = [], []
    for values, picks in pairs:
        operands += [values, picks]
        specs.append(pl.BlockSpec((count, block, values.shape[2]), lambda i: (0, i, 0)))
        specs.append(pl.BlockSpec(picks.shape, lambda i: (0, 0)))
    for whole in (rotations, scale):
        operands.append(whole)
        specs.append(pl.BlockSpec(whole.shape, lambda i: (0, 0)))
    return pl.pallas_call(
        frames_kernel,
        grid=(local // block,),
        in_specs=specs,
        out_specs=pl.BlockSpec((len(FRAME), block, edges), lambda i: (0, i, 0)),
        out_shape=jax.ShapeDtypeStruct((len(FRAME), local, edges), jnp.bfloat16),
        compiler_params=pltpu.CompilerParams(dimension_semantics=("arbitrary",)),
    )(*operands)


def atoms_kernel(count, values, rotations, scale, *refs):
    picks, outs, held = refs[: len(refs) // 2], refs[len(refs) // 2 : -1], refs[-1]
    width, edges = values.shape[1], values.shape[2]
    for degree in range(5):
        members = [row for row, pair in enumerate(FRAME) if pair[0] == degree]
        lines = [values[row].astype(jnp.float32) * scale[...] for row in members]
        for column in range(degree * degree, (degree + 1) * (degree + 1)):
            total = None
            for row, line in zip(members, lines):
                entry = row * count + column
                term = rotations[entry : entry + 1, :] * line
                total = term if total is None else total + term
            held[column] = total.astype(held.dtype)
    flat = held[...].reshape(count * width, edges)
    for pick, out in zip(picks, outs):
        out[...] = product(flat, pick[...]).reshape(out.shape).astype(out.dtype)


def to_atoms(values, rotations, scale, picks, kinds):
    rows, local, edges = values.shape
    count = rotations.shape[0] // rows
    block = min(64, local)
    whole = lambda i: (0, 0)
    return pl.pallas_call(
        functools.partial(atoms_kernel, count),
        grid=(local // block,),
        in_specs=[
            pl.BlockSpec((rows, block, edges), lambda i: (0, i, 0)),
            pl.BlockSpec(rotations.shape, whole),
            pl.BlockSpec(scale.shape, whole),
        ]
        + [pl.BlockSpec(pick.shape, whole) for pick in picks],
        out_specs=[
            pl.BlockSpec((count, block, pick.shape[1]), lambda i: (0, i, 0)) for pick in picks
        ],
        out_shape=[
            jax.ShapeDtypeStruct((count, local, pick.shape[1]), kind)
            for pick, kind in zip(picks, kinds)
        ],
        scratch_shapes=[pltpu.VMEM((count, block, edges), jnp.bfloat16)],
        compiler_params=pltpu.CompilerParams(dimension_semantics=("arbitrary",)),
    )(values, rotations, scale, *picks)


def swap(block, bit):
    count = lax.axis_size("graph")
    return lax.ppermute(block, "graph", [(i, i ^ bit) for i in range(count)])


def from_beside(faces, width):
    count = lax.axis_size("graph")
    forward = [(i, (i + 1) % count) for i in range(count)]
    backward = [(target, source) for source, target in forward]
    low = lax.ppermute(faces[:, :, width:], "graph", forward)
    high = lax.ppermute(faces[:, :, :width], "graph", backward)
    return jnp.concatenate([low, high], axis=2)


def hot_rows(size, codes):
    return (jnp.arange(size, dtype=jnp.int32)[:, None] == codes[None, :]).astype(jnp.bfloat16)


def hot_columns(codes, size):
    return (codes[:, None] == jnp.arange(size, dtype=jnp.int32)[None, :]).astype(jnp.bfloat16)


def beside(plus, minus, axis=-1):
    return jnp.concatenate([plus, minus], axis=axis)


def mix_forward(weights, frame):
    w_zero, w_one, w_two = weights
    edges = frame.shape[2]
    local = w_zero.shape[1]
    mixed = [
        product(w_zero.reshape(-1, w_zero.shape[2]), frame[:5].reshape(-1, edges)).reshape(
            5, local, edges
        )
    ]
    for weight, first, blocks in ((w_one, 5, 4), (w_two, 13, 3)):
        plus = frame[first : first + blocks].reshape(-1, edges)
        minus = frame[first + blocks : first + 2 * blocks].reshape(-1, edges)
        both = product(weight.reshape(-1, weight.shape[-1]), beside(plus, minus))
        both = both.reshape(2, blocks, local, 2 * edges)
        mixed.append(both[0, :, :, :edges] - both[1, :, :, edges:])
        mixed.append(both[0, :, :, edges:] + both[1, :, :, :edges])
    return jnp.concatenate(mixed, axis=0)


def mix_back(weights, grads, shares):
    w_zero, w_one, w_two = weights
    edges = grads.shape[2]

    def shared(block, blocks):
        shaped = block.reshape(blocks, shares, -1, edges).astype(jnp.bfloat16)
        return jnp.transpose(shaped, (1, 0, 2, 3))

    back = [
        shared(across(w_zero.reshape(-1, w_zero.shape[2]), grads[:5].reshape(-1, edges)), 5)
    ]
    for weight, first, blocks in ((w_one, 5, 4), (w_two, 13, 3)):
        plus = grads[first : first + blocks].reshape(-1, edges)
        minus = grads[first + blocks : first + 2 * blocks].reshape(-1, edges)
        sides = jnp.concatenate([beside(plus, minus), beside(minus, -plus)], axis=0)
        both = across(weight.reshape(-1, weight.shape[-1]), sides)
        back.append(shared(both[:, :edges], blocks))
        back.append(shared(both[:, edges:], blocks))
    return jnp.concatenate(back, axis=1)


def column_frames(frame):
    count = lax.axis_size("graph")
    near = 4
    far = count // near
    edges = frame.shape[2]
    cuts = ((0, 5), (5, 4), (9, 4), (13, 3), (16, 3))
    parts = [
        frame[first : first + blocks].reshape(far, near, -1, edges) for first, blocks in cuts
    ]
    widths = [part.shape[2] for part in parts]
    packed = jnp.concatenate(parts, axis=2)
    mine = lax.axis_index("graph") % near
    frames = []
    for bit in (0, 2, 1, 3):
        target = mine ^ bit
        chunk = lax.dynamic_index_in_dim(packed, target, axis=1, keepdims=False)
        frames.append(swap(chunk, bit) if bit else chunk)
    return frames, widths


def weight_grads(frames, widths, grads_all, local):
    count = lax.axis_size("graph")
    near = 4
    far = count // near
    edges = frames[0].shape[2]
    starts = [sum(widths[:i]) for i in range(5)]
    groups = [[z * near + q for z in range(far)] for q in range(near)]

    def settle(partial):
        return lax.psum_scatter(
            partial.astype(jnp.bfloat16),
            "graph",
            scatter_dimension=0,
            axis_index_groups=groups,
            tiled=False,
        ).astype(jnp.float32)

    def settle_direct(partial):
        partial = partial.astype(jnp.bfloat16)
        place = lax.axis_index("graph") // near
        total = lax.dynamic_index_in_dim(partial, place, axis=0, keepdims=False)
        total = total.astype(jnp.float32)
        for step in range(1, far):
            chunk = lax.dynamic_index_in_dim(partial, (place + step) % far, axis=0, keepdims=False)
            shift = [(i, (i + step * near) % count) for i in range(count)]
            total = total + lax.ppermute(chunk, "graph", shift).astype(jnp.float32)
        return total

    def columns(index):
        return [chunk[:, starts[index] : starts[index] + widths[index]] for chunk in frames]

    left = jnp.concatenate(columns(0), axis=2)
    right = jnp.concatenate([g[:5].reshape(-1, edges) for g in grads_all], axis=1)
    done = settle_direct(contract(left, right))
    results = [jnp.transpose(done).reshape(5, local, widths[0])]
    for index, first, blocks in ((1, 5, 4), (3, 13, 3)):
        plus, minus = columns(index), columns(index + 1)
        real_part = jnp.concatenate([x for pair in zip(plus, minus) for x in pair], axis=2)
        imag_part = jnp.concatenate([x for pair in zip(minus, plus) for x in (-pair[0], pair[1])], axis=2)
        left = jnp.concatenate([real_part, imag_part], axis=1)
        right = jnp.concatenate(
            [
                g[start : start + blocks].reshape(-1, edges)
                for g in grads_all
                for start in (first, first + blocks)
            ],
            axis=1,
        )
        done = settle(contract(left, right))
        done = done.reshape(2, widths[index], blocks * local)
        results.append(jnp.transpose(done, (0, 2, 1)).reshape(2, blocks, local, widths[index]))
    return results


def shards(
    embed,
    gain,
    w_zero,
    w_one,
    w_two,
    rot_table,
    face_atoms,
    edge_source,
    edge_target,
    rot_index,
    edge_weight,
    cotangent,
):
    atoms = embed.shape[2]
    local = embed.shape[1]
    halo = face_atoms.shape[0] // 2
    shares = lax.axis_size("chan")
    channels = local * shares
    weights = (w_zero, w_one, w_two)
    values = embed.astype(jnp.float32)
    gains = gain_rows(gain)
    rows, coefficients, rots = rot_table.shape
    which = (jnp.arange(rots, dtype=jnp.int32)[:, None] == rot_index[None, :]).astype(jnp.float32)
    rotations = jnp.dot(
        rot_table.reshape(rows * coefficients, rots),
        which,
        precision=HIGHEST,
        preferred_element_type=jnp.float32,
    )
    weight_row = edge_weight[None, :]
    ones = jnp.ones_like(weight_row)

    squares = lax.psum(jnp.sum(values * values, axis=(0, 1)), "chan")
    inverse = lax.rsqrt(squares / (25 * channels) + EPSILON)
    normed = (values * inverse[None, None, :] * gains[:, :, None]).astype(jnp.bfloat16)
    flat = normed.reshape(25 * local, atoms)
    faces = product(flat, hot_rows(atoms, face_atoms)).astype(jnp.bfloat16)
    table_end = from_beside(faces.reshape(25, local, 2 * halo), halo)

    grads = to_frames([(cotangent, hot_rows(atoms, edge_target))], rotations, weight_row)
    picks = hot_rows(atoms + 2 * halo, edge_source)
    own = to_frames([(normed, picks[:atoms]), (table_end, picks[atoms:])], rotations, ones)
    own, grads = lax.optimization_barrier((own, grads))
    piece = lax.all_gather(own, "chan", axis=1, tiled=True)

    grads_side = swap(grads, 2)
    pair = swap(jnp.stack([grads, grads_side]), 1)
    grads_all = [grads, grads_side, pair[0], pair[1]]

    back = lax.psum_scatter(
        mix_back(weights, grads, shares), "chan", scatter_dimension=0, tiled=False
    )
    frames, widths = column_frames(piece)
    mixed = mix_forward(weights, piece)
    mixed, frames = lax.optimization_barrier((mixed, frames))
    (update,) = to_atoms(
        mixed, rotations, weight_row, [hot_columns(edge_target, atoms)], [jnp.bfloat16]
    )
    leaving = hot_columns(edge_source, atoms + 2 * halo)
    mine, outward = to_atoms(
        back,
        rotations,
        ones,
        [leaving[:, :atoms], leaving[:, atoms:]],
        [jnp.float32, jnp.bfloat16],
    )
    incoming = from_beside(outward, halo)
    settled = product(incoming.reshape(25 * local, 2 * halo), hot_columns(face_atoms, atoms))
    grad_normed = mine + settled.reshape(25, local, atoms)
    scaled = inverse[None, None, :] * gains[:, :, None] * grad_normed
    tally = lax.psum(jnp.sum(values * scaled, axis=(0, 1)), "chan")
    grad_embed = (
        scaled
        - values * (inverse**2 * tally / (25 * channels))[None, None, :]
    ).astype(jnp.bfloat16)
    grad_zero, grad_one, grad_two = weight_grads(frames, widths, grads_all, local)
    return (update, grad_embed, grad_zero, grad_one, grad_two)


def solution(mesh):
    placed = (
        P(None, "chan", "graph"),
        P(None, "chan"),
        P(None, "chan", None),
        P(None, None, "chan", None),
        P(None, None, "chan", None),
        P(),
        P("graph"),
        P("graph"),
        P("graph"),
        P("graph"),
        P("graph"),
        P(None, "chan", "graph"),
    )
    return jax.shard_map(
        shards,
        mesh=mesh,
        in_specs=placed,
        out_specs=(
            P(None, "chan", "graph"),
            P(None, "chan", "graph"),
            P(None, "chan", "graph"),
            P(None, None, "chan", "graph"),
            P(None, None, "chan", "graph"),
        ),
        check_vma=False,
    )
```

time: 833 us -> 270 us (0.32)
  the two profiles are of different devices: /device:TPU:0 before, /device:TPU:4 now
where the time goes in v1:
time: 270 us; the launch traced here: 268 us
  local copies, waits for them, and re-layouts  78.1 us (29%)
  waiting for transfers between devices  71.8 us (27%)
  matrix products  43 us (16%)
  other arithmetic  20.6 us (8%)
  Pallas kernels  19.3 us (7%)
  between operations  14.7 us (5%)
  starting transfers between devices  11.1 us (4%)
  blocking collectives  9.84 us (4%)
    ppermute x3, waiting for transfers between devices, settle_direct(): total = total + lax.ppermute(chunk, 'graph', shift).astype(jnp.float32)  46.3 us
    ppermute x5, waiting for transfers between devices, swap(): return lax.ppermute(block, 'graph', [(i, i ^ bit) for i in range(count)])  25.3 us
    unnamed x110, local copies, waits for them, and re-layouts  25.1 us
    dot_general x5, matrix products, product(): return jnp.dot(left, right, preferred_element_type=jnp.float32)  22.3 us
    dot_general x3, matrix products, across(): lax.dot_general(left, right, (((0,), (0,)), ((), ())), preferred_element_...  11 us
    pallas_call x2, Pallas kernels, to_atoms(): pl.pallas_call(functools.partial(atoms_kernel, count), grid=(local // blo...  9.95 us
    pallas_call x2, Pallas kernels, to_frames(): pl.pallas_call(frames_kernel, grid=(local // block,), in_specs=specs, out...  9.35 us
    dot_general x3, matrix products, contract(): lax.dot_general(left, right, (((2,), (1,)), ((), ())), preferred_element_...  8.61 us
  transfers between devices with their start and end apart: 16, of which 4 were waited for; matrix products, arithmetic and copies ran while one was open for 45% of the time, Pallas kernels for 5%

profile of v1, /device:TPU:4, one launch (start us, length us, event | category | flops | bytes accessed | tf_op | source)
XLA Modules:
  0.0 268.4 jit_solution(1271034299307463333)
XLA Ops:
  8.1 2.3 fusion.2
  10.4 4.9 %psum.14 = f32[128]{0:T(128)S(1)} all-reduce(f32[128]{0:T(128)S(1)} %fusion.2), channel_id=1, replica_groups=mesh['graph'=16,'chan'=2] {'chan'}, use_global_device_ids=true, to_apply=%region_1.0 | all-reduce | flops 128 | bytes 1024 | tf_op jit(solution)/shard_map/psum | solution.py:315
  16.6 1.5 convolution_convert_fusion
  18.0 2.0 reshape.209
  26.4 4.5 %shard_map.156 = bf16[19,256,128]{2,1,0:T(8,128)(2,1)} custom-call(bf16[25,256,128]{2,1,0:T(8,128)(2,1)} %refs_0_.1, bf16[128,128]{1,0:T(8,128)(2,1)} %get-tuple-element.118.refs_1_, f32[475,128]{1,0:T(8,128)} %convolution_bitcast_fusion.4.refs_4_.refs_2_.rotations, f32[1,128]{1,0:T(1,128)} %bitcast.223), custom_call_target="tpu_custom_call" | custom-call | tf_op jit(solution)/shard_map/pallas_call | solution.py:88
  31.8 1.6 copy.71.refs_2_
  33.9 4.9 %shard_map.155 = bf16[19,256,128]{2,1,0:T(8,128)(2,1)} custom-call(bf16[25,256,128]{2,1,0:T(8,128)(2,1)} %copy-done.1, bf16[128,128]{1,0:T(8,128)(2,1)} %slice.316.refs_1_, bf16[25,256,32]{2,1,0:T(8,128)(2,1)} %copy.71.refs_2_, bf16[32,128]{1,0:T(8,128)(2,1)} %slice.319.refs_3_, f32[475,128]{1,0:T(8,128)} %convolution_bitcast_fusion.4.refs_4_.refs_2_.rotations, ...), custom_call_target="tpu_custom_call" | custom-call | tf_op jit(solution)/shard_map/pallas_call | solution.py:88
  39.8 2.9 %collective-permute-start.7 = (bf16[19,256,128]{2,1,0:T(8,128)(2,1)S(1)}, bf16[19,256,128]{2,1,0:T(8,128)(2,1)}, u32[]{:S(2)}, u32[]{:S(2)}) collective-permute-start(bf16[19,256,128]{2,1,0:T(8,128)(2,1)S(1)} %copy-done.2), channel_id=1, source_target_pairs={{0,4},{2,6},{4,0},{6,2},{8,12},{10,14},{12,8},{14,10},{16,20},{18,... | collective-permute-start | bytes 3735560 | tf_op jit(solution)/shard_map/ppermute | solution.py:144
  42.8 5.9 %fusion.8 = bf16[2048,256]{0,1:T(8,128)(2,1)S(1)} fusion(bf16[2048,2048]{1,0:T(8,128)(2,1)} %bitcast.225, bf16[1024,128]{1,0:T(8,128)(2,1)S(1)} %bitcast_negate_fusion.1, bf16[1024,128]{1,0:T(8,128)(2,1)S(1)} %bitcast.195, bf16[1024,128]{1,0:T(8,128)(2,1)S(1)} %bitcast.177), kind=kOutput, calls=%fused_computation.21 | convolution fusion | flops 2152202240 | bytes 10223616 | tf_op jit(solution)/shard_map/dot_general | solution.py:49
  51.9 1.3 copy.78
  54.2 2.1 bitcast_dynamic-update-slice_fusion
  56.3 4.0 %fusion.9 = bf16[1536,256]{0,1:T(8,128)(2,1)S(1)} fusion(bf16[1536,1536]{1,0:T(8,128)(2,1)} %bitcast.227, bf16[768,128]{1,0:T(8,128)(2,1)S(1)} %bitcast_negate_fusion, bf16[768,128]{1,0:T(8,128)(2,1)} %bitcast.208, bf16[768,128]{1,0:T(8,128)(2,1)} %bitcast.185), kind=kOutput, calls=%fused_computation.22 | convolution fusion | flops 1211498496 | bytes 6094848 | tf_op jit(solution)/shard_map/dot_general | solution.py:49
  62.2 1.3 copy.80
  63.5 1.9 copy.82
  65.4 1.9 copy.84
  68.3 1.9 bitcast_dynamic-update-slice_fusion.4
  73.8 3.0 %pad_maximum_fusion = bf16[2,19,256,128]{3,2,1,0:T(8,128)(2,1)} fusion(bf16[1,19,256,128]{3,2,1,0:T(8,128)(2,1)} %bitcast.57, bf16[1,19,256,128]{3,2,1,0:T(8,128)(2,1)S(1)} %bitcast.166), kind=kLoop, calls=%fused_computation.20 | loop fusion | flops 1245184 | bytes 4980736 | tf_op jit(solution)/shard_map/stack | solution.py:329
  78.1 1.5 fusion.99
  82.3 5.9 %convolution_bitcast_fusion.3 = f32[1280,128]{0,1:T(8,128)} fusion(bf16[2560,128]{1,0:T(8,128)(2,1)S(1)} %bitcast.171, bf16[1280,2560]{1,0:T(8,128)(2,1)} %bitcast.162), kind=kOutput, calls=%fused_computation.23 | convolution fusion | flops 838860800 | bytes 7864320 | tf_op jit(solution)/shard_map/dot_general | solution.py:45
  88.3 2.2 copy.72
  90.4 1.3 fusion.97
  92.8 7.1 %convolution_bitcast_fusion.2 = f32[2048,256]{0,1:T(8,128)} fusion(bf16[2048,2048]{1,0:T(8,128)(2,1)} %bitcast.226, bf16[2048,128]{1,0:T(8,128)(2,1)S(1)} %bitcast.181, bf16[2048,128]{1,0:T(8,128)(2,1)S(1)} %bitcast.183), kind=kOutput, calls=%fused_computation.17 | convolution fusion | flops 2149580800 | bytes 11534336 | tf_op jit(solution)/shard_map/dot_general | solution.py:45
  99.8 2.9 %copy.73 = f32[2048,256]{1,0:T(8,128)} copy(f32[2048,256]{0,1:T(8,128)} %convolution_bitcast_fusion.2) | data formatting | bytes 4194304 | tf_op jit(solution)/shard_map/dot_general | solution.py:45
  104.8 5.0 %convolution_bitcast_fusion.1 = f32[1536,256]{0,1:T(8,128)} fusion(bf16[1536,1536]{1,0:T(8,128)(2,1)} %bitcast.228, bf16[1536,128]{1,0:T(8,128)(2,1)S(1)} %bitcast.189, bf16[1536,128]{1,0:T(8,128)(2,1)S(1)} %bitcast.191), kind=kOutput, calls=%fused_computation.16 | convolution fusion | flops 1209532416 | bytes 7077888 | tf_op jit(solution)/shard_map/dot_general | solution.py:45
  109.8 3.0 %copy.74 = f32[1536,256]{1,0:T(8,128)} copy(f32[1536,256]{0,1:T(8,128)} %convolution_bitcast_fusion.1) | data formatting | bytes 3145728 | tf_op jit(solution)/shard_map/dot_general | solution.py:45
  115.2 1.6 collective-permute-start.4
  118.3 13.2 %collective-permute-done.2 = bf16[4,608,128]{2,1,0:T(8,128)(2,1)S(1)} collective-permute-done((bf16[4,608,128]{2,1,0:T(8,128)(2,1)S(1)}, bf16[4,608,128]{2,1,0:T(8,128)(2,1)S(1)}, u32[]{:S(2)}, u32[]{:S(2)}) %collective-permute-start.2) | collective-permute-done | bytes 622624 | tf_op jit(solution)/shard_map/ppermute | solution.py:144
  131.5 12.0 %collective-permute-done.4 = bf16[4,608,128]{2,1,0:T(8,128)(2,1)S(1)} collective-permute-done((bf16[4,608,128]{2,1,0:T(8,128)(2,1)S(1)}, bf16[4,608,128]{2,1,0:T(8,128)(2,1)S(1)}, u32[]{:S(2)}, u32[]{:S(2)}) %collective-permute-start.4) | collective-permute-done | bytes 622624 | tf_op jit(solution)/shard_map/ppermute | solution.py:144
  150.5 3.8 %fusion.25 = bf16[4,192,768]{2,1,0:T(8,128)(2,1)} fusion(bf16[768,1024]{1,0:T(8,128)(2,1)} %constant_dynamic-update-slice_fusion.46, bf16[4,96,1024]{2,1,0:T(8,128)(2,1)S(1)} %get-tuple-element.79, bf16[4,96,1024]{2,1,0:T(8,128)(2,1)S(1)} %get-tuple-element.78), kind=kOutput, calls=%fused_computation.35 | convolution fusion | flops 1211695104 | bytes 4325376 | tf_op jit(solution)/shard_map/dot_general | solution.py:55
  154.6 1.8 constant_dynamic-update-slice_fusion.10
  156.4 1.8 constant_dynamic-update-slice_fusion.9
  158.2 1.7 constant_dynamic-update-slice_fusion.8
  159.9 1.7 constant_dynamic-update-slice_fusion.7
  162.3 1.4 fusion.94
  164.2 3.7 %fusion.15 = bf16[4,256,1024]{2,1,0:T(8,128)(2,1)} fusion(bf16[1024,1024]{1,0:T(8,128)(2,1)S(1)} %constant_dynamic-update-slice_fusion.22, bf16[4,128,1024]{2,1,0:T(8,128)(2,1)S(1)} %copy-done.33, bf16[4,128,1024]{2,1,0:T(8,128)(2,1)S(1)} %copy-done.31), kind=kOutput, calls=%fused_computation.29 | convolution fusion | flops 2152726528 | bytes 6291456 | tf_op jit(solution)/shard_map/dot_general | solution.py:55
  173.6 2.9 %collective-permute-start.11 = (bf16[160,1280]{1,0:T(8,128)(2,1)}, bf16[160,1280]{1,0:T(8,128)(2,1)}, u32[]{:S(2)}, u32[]{:S(2)}) collective-permute-start(bf16[160,1280]{1,0:T(8,128)(2,1)} %get-tuple-element.62), channel_id=1, source_target_pairs={{0,24},{2,26},{4,28},{6,30},{8,0},{10,2},{12,4},{14,6},{16,8},{18,... | collective-permute-start | bytes 1228808 | tf_op jit(solution)/shard_map/ppermute | solution.py:253
  178.4 4.8 %shard_map.157 = bf16[25,256,128]{2,1,0:T(8,128)(2,1)} custom-call(f32[19,256,128]{2,1,0:T(8,128)} %copy-done.5, f32[475,128]{1,0:T(8,128)} %convolution_bitcast_fusion.4.refs_4_.refs_2_.rotations, f32[1,128]{1,0:T(1,128)} %bitcast.224, bf16[128,128]{1,0:T(8,128)(2,1)} %get-tuple-element.117.refs_0_), custom_call_target="tpu_custom_call" | custom-call | tf_op jit(solution)/shard_map/pallas_call | solution.py:121
  183.2 5.2 %shard_map.158 = (f32[25,256,128]{2,1,0:T(8,128)}, bf16[25,256,32]{2,1,0:T(8,128)(2,1)}) custom-call(bf16[19,256,128]{2,1,0:T(8,128)(2,1)} %bitcast.193, f32[475,128]{1,0:T(8,128)} %convolution_bitcast_fusion.4.refs_4_.refs_2_.rotations, f32[1,128]{1,0:T(1,128)} %broadcast_in_dim.28.refs_5_.scale, bf16[128,128]{1,0:T(8,128)(2,1)} %slice.337.refs_0_, ...), custom_call_target="tpu_custom_call" | custom-call | tf_op jit(solution)/shard_map/pallas_call | solution.py:121
  188.4 3.8 %fusion.98 = (bf16[25,256,16]{2,1,0:T(8,128)(2,1)S(1)}, bf16[25,256,16]{2,1,0:T(8,128)(2,1)}) fusion(bf16[25,256,32]{2,1,0:T(8,128)(2,1)} %get-tuple-element.18), kind=kLoop, calls=%fused_computation.191 | loop fusion | bytes 819200 | tf_op jit(solution)/shard_map/slice | solution.py:151
  192.2 2.3 copy.87
  194.6 1.3 collective-permute-start.6
  195.9 1.3 copy.86
  197.3 46.3 %collective-permute-done.10 = bf16[160,1280]{1,0:T(8,128)(2,1)} collective-permute-done((bf16[160,1280]{1,0:T(8,128)(2,1)}, bf16[160,1280]{1,0:T(8,128)(2,1)}, u32[]{:S(2)}, u32[]{:S(2)}) %collective-permute-start.10) | collective-permute-done | bytes 409632 | tf_op jit(solution)/shard_map/ppermute | solution.py:253
  243.6 1.6 fusion.47
  246.1 2.8 %fusion.5 = (f32[128]{0:T(128)S(1)}, f32[25,256,128]{2,1,0:T(8,128)}) fusion(bf16[25,256,128]{2,1,0:T(8,128)(2,1)S(1)} %copy-done, f32[25,256,128]{2,1,0:T(8,128)S(1)} %copy-done.6, s32[32]{0:T(128)S(1)} %copy-done.35, bf16[25,256,16]{1,2,0:T(8,128)(2,1)S(1)} %collective-permute-done.6, bf16[25,256,16]{1,2,0:T(8,128)(2,1)S(1)} %collective-permute-done.5, ...), kind=kOutput, calls=%fused_computation.11 | convolution fusion | flops 58167168 | bytes 8628352 | tf_op jit(solution)/shard_map/dot_general | solution.py:45
  249.0 4.9 %psum.15 = f32[128]{0:T(128)S(1)} all-reduce(f32[128]{0:T(128)S(1)} %get-tuple-element.119), channel_id=1, replica_groups=mesh['graph'=16,'chan'=2] {'chan'}, use_global_device_ids=true, to_apply=%region_4.5 | all-reduce | flops 128 | bytes 1024 | tf_op jit(solution)/shard_map/psum | solution.py:353
  253.9 3.6 %fusion.7 = bf16[25,256,128]{2,1,0:T(8,128)(2,1)} fusion(f32[25,256,128]{2,1,0:T(8,128)} %get-tuple-element.120, bf16[25,256,128]{2,1,0:T(8,128)(2,1)S(1)} %copy-done, f32[128]{0:T(128)S(1)} %multiply_multiply_fusion), kind=kLoop, calls=%fused_computation.13 | loop fusion | flops 3276800 | bytes 6554112 | tf_op jit(solution)/shard_map/convert_element_type | solution.py:357
  260.5 1.3 copy.88
  (204 shorter events, 51.9 us)
Async XLA Ops:
  7.2 8.3 %copy-start = (bf16[25,256,128]{2,1,0:T(8,128)(2,1)S(1)}, bf16[25,256,128]{2,1,0:T(8,128)(2,1)}, u32[]{:S(2)}) copy-start(bf16[25,256,128]{2,1,0:T(8,128)(2,1)} %param.12) | copy-start | bytes 4915204
  7.2 74.0 %all-gather.2.cloned.1.call-start = ((), (), s32[]{:S(2)}) async-start(), calls=%async_computation.3 | async-start | bytes 3735552 | tf_op jit(solution)/shard_map/all_gather | solution.py:326
  10.4 6.1 %copy-start.35 = (s32[32]{0:T(128)S(1)}, s32[32]{0:T(128)}, u32[]{:S(2)}) copy-start(s32[32]{0:T(128)} %param.18) | copy-start | bytes 388
  15.5 2.5 copy-start.26
  16.5 4.7 %copy-start.1 = (bf16[25,256,128]{2,1,0:T(8,128)(2,1)}, bf16[25,256,128]{2,1,0:T(8,128)(2,1)S(1)}, u32[]{:S(2)}) copy-start(bf16[25,256,128]{2,1,0:T(8,128)(2,1)S(1)} %fusion.4.refs_0_) | copy-start | bytes 4915204
  16.6 5.4 %copy-start.36 = (s32[128]{0:T(128)S(1)}, s32[128]{0:T(128)}, u32[]{:S(2)}) copy-start(s32[128]{0:T(128)} %param.19) | copy-start | bytes 1540
  20.0 4.5 %copy-start.37 = (s32[128]{0:T(128)S(1)}, s32[128]{0:T(128)}, u32[]{:S(2)}) copy-start(s32[128]{0:T(128)} %param.21) | copy-start | bytes 1540
  21.1 4.6 %copy-start.34 = (s32[128]{0:T(128)S(1)}, s32[128]{0:T(128)}, u32[]{:S(2)}) copy-start(s32[128]{0:T(128)} %param.20) | copy-start | bytes 1540
  21.3 9.6 %collective-permute-start.1 = (bf16[25,256,16]{1,2,0:T(8,128)(2,1)S(1)}, bf16[25,256,16]{1,2,0:T(8,128)(2,1)}, u32[]{:S(2)}, u32[]{:S(2)}) collective-permute-start(bf16[25,256,16]{1,2,0:T(8,128)(2,1)S(1)} %copy.69), channel_id=1, source_target_pairs={{2,0},{4,2},{6,4},{8,6},{10,8},{12,10},{14,12},{16,14},{18,16},{20... | collective-permute-start | bytes 614408 | tf_op jit(solution)/shard_map/ppermute | solution.py:152
  21.5 9.4 %collective-permute-start = (bf16[25,256,16]{1,2,0:T(8,128)(2,1)S(1)}, bf16[25,256,16]{1,2,0:T(8,128)(2,1)S(1)}, u32[]{:S(2)}, u32[]{:S(2)}) collective-permute-start(bf16[25,256,16]{1,2,0:T(8,128)(2,1)S(1)} %copy.68), channel_id=1, source_target_pairs={{0,2},{2,4},{4,6},{6,8},{8,10},{10,12},{12,14},{14,16},{16,18},{18... | collective-permute-start | bytes 614408 | tf_op jit(solution)/shard_map/ppermute | solution.py:151
  33.9 4.9 %copy-start.2 = (bf16[19,256,128]{2,1,0:T(8,128)(2,1)S(1)}, bf16[19,256,128]{2,1,0:T(8,128)(2,1)}, u32[]{:S(2)}) copy-start(bf16[19,256,128]{2,1,0:T(8,128)(2,1)} %shard_map.156) | copy-start | bytes 3735556
  38.9 9.8 %copy-start.8 = (bf16[4,256,128]{2,1,0:T(8,128)(2,1)}, bf16[4,256,128]{2,1,0:T(8,128)(2,1)S(1)}, u32[]{:S(2)}) copy-start(bf16[4,256,128]{2,1,0:T(8,128)(2,1)S(1)} %get-tuple-element.73) | copy-start | bytes 786436
  38.9 9.8 %copy-start.24 = (bf16[4,256,128]{2,1,0:T(8,128)(2,1)}, bf16[4,256,128]{2,1,0:T(8,128)(2,1)S(1)}, u32[]{:S(2)}) copy-start(bf16[4,256,128]{2,1,0:T(8,128)(2,1)S(1)} %get-tuple-element.72) | copy-start | bytes 786436
  39.8 34.0 %collective-permute-start.7 = (bf16[19,256,128]{2,1,0:T(8,128)(2,1)S(1)}, bf16[19,256,128]{2,1,0:T(8,128)(2,1)}, u32[]{:S(2)}, u32[]{:S(2)}) collective-permute-start(bf16[19,256,128]{2,1,0:T(8,128)(2,1)S(1)} %copy-done.2), channel_id=1, source_target_pairs={{0,4},{2,6},{4,0},{6,2},{8,12},{10,14},{12,8},{14,10},{16,20},{18,... | collective-permute-start | bytes 3735560 | tf_op jit(solution)/shard_map/ppermute | solution.py:144
  42.6 140.6 %reduce-scatter.4.cloned.1.call-start = ((), (), s32[]{:S(2)}) async-start(), calls=%async_computation.4 | async-start | bytes 3735552 | tf_op jit(solution)/shard_map/reduce_scatter | solution.py:332
  42.7 7.0 %slice-start = ((s8[6553600]{0:T(1024)(128)(4,1)}), s8[4194304]{0:T(1024)(128)(4,1)S(1)}, s32[]{:S(2)}) async-start(s8[6553600]{0:T(1024)(128)(4,1)} %bitcast.163), calls=%async_computation.7 | async-start | bytes 8388608
  42.8 7.0 %slice-start.1 = ((s8[6553600]{0:T(1024)(128)(4,1)}), s8[2359296]{0:T(1024)(128)(4,1)S(1)}, s32[]{:S(2)}) async-start(s8[6553600]{0:T(1024)(128)(4,1)} %bitcast.163), calls=%async_computation.8 | async-start | bytes 4718592
  67.4 2.8 %copy-start.19 = (bf16[1536,128]{1,0:T(8,128)(2,1)S(1)}, bf16[1536,128]{1,0:T(8,128)(2,1)}, u32[]{:S(2)}) copy-start(bf16[1536,128]{1,0:T(8,128)(2,1)} %copy.84) | copy-start | bytes 1179652
  68.3 2.9 %copy-start.17 = (bf16[3,256,128]{2,1,0:T(8,128)(2,1)S(1)}, bf16[3,256,128]{2,1,0:T(8,128)(2,1)}, u32[]{:S(2)}) copy-start(bf16[3,256,128]{2,1,0:T(8,128)(2,1)} %get-tuple-element.71) | copy-start | bytes 589828
  68.3 3.7 %copy-start.25 = (bf16[3,256,128]{2,1,0:T(8,128)(2,1)S(1)}, bf16[3,256,128]{2,1,0:T(8,128)(2,1)}, u32[]{:S(2)}) copy-start(bf16[3,256,128]{2,1,0:T(8,128)(2,1)} %get-tuple-element.70) | copy-start | bytes 589828
  70.1 2.6 copy-start.9
  71.0 186.5 %reduce-scatter.8.cloned.1.call-start = ((), (), s32[]{:S(2)}) async-start(), calls=%async_computation.6 | async-start | bytes 1474560 | tf_op jit(solution)/shard_map/reduce_scatter | solution.py:237
  76.8 69.5 %collective-permute-start.8 = (bf16[2,19,256,128]{3,2,1,0:T(8,128)(2,1)}, bf16[2,19,256,128]{3,2,1,0:T(8,128)(2,1)}, u32[]{:S(2)}, u32[]{:S(2)}) collective-permute-start(bf16[2,19,256,128]{3,2,1,0:T(8,128)(2,1)} %pad_maximum_fusion), channel_id=1, source_target_pairs={{0,2},{2,0},{4,6},{6,4},{8,10},{10,8},{12,14},{14,12},{16,18},{18,... | collective-permute-start | bytes 7471112 | tf_op jit(solution)/shard_map/ppermute | solution.py:144
  78.1 2.3 copy-start.28
  112.8 1.5 copy-start.21
  114.3 2.4 copy-start.7
  114.4 2.5 copy-start.3
  114.5 17.0 %collective-permute-start.2 = (bf16[4,608,128]{2,1,0:T(8,128)(2,1)S(1)}, bf16[4,608,128]{2,1,0:T(8,128)(2,1)S(1)}, u32[]{:S(2)}, u32[]{:S(2)}) collective-permute-start(bf16[4,608,128]{2,1,0:T(8,128)(2,1)S(1)} %get-tuple-element.55), channel_id=1, source_target_pairs={{0,4},{2,6},{4,0},{6,2},{8,12},{10,14},{12,8},{14,10},{16,20},{18,... | collective-permute-start | bytes 1867784 | tf_op jit(solution)/shard_map/ppermute | solution.py:144
  115.2 16.3 %collective-permute-start.3 = (bf16[4,608,128]{2,1,0:T(8,128)(2,1)S(1)}, bf16[4,608,128]{2,1,0:T(8,128)(2,1)S(1)}, u32[]{:S(2)}, u32[]{:S(2)}) collective-permute-start(bf16[4,608,128]{2,1,0:T(8,128)(2,1)S(1)} %get-tuple-element.54), channel_id=1, source_target_pairs={{0,2},{2,0},{4,6},{6,4},{8,10},{10,8},{12,14},{14,12},{16,18},{18,... | collective-permute-start | bytes 1867784 | tf_op jit(solution)/shard_map/ppermute | solution.py:144
  115.2 28.4 %collective-permute-start.4 = (bf16[4,608,128]{2,1,0:T(8,128)(2,1)S(1)}, bf16[4,608,128]{2,1,0:T(8,128)(2,1)S(1)}, u32[]{:S(2)}, u32[]{:S(2)}) collective-permute-start(bf16[4,608,128]{2,1,0:T(8,128)(2,1)S(1)} %get-tuple-element.53), channel_id=1, source_target_pairs={{0,6},{2,4},{4,2},{6,0},{8,14},{10,12},{12,10},{14,8},{16,22},{18,... | collective-permute-start | bytes 1867784 | tf_op jit(solution)/shard_map/ppermute | solution.py:144
  118.3 26.0 %copy-start.5 = (f32[19,256,128]{2,1,0:T(8,128)}, f32[19,256,128]{2,1,0:T(8,128)S(1)}, u32[]{:S(2)}) copy-start(f32[19,256,128]{2,1,0:T(8,128)S(1)} %fusion.73.values) | copy-start | bytes 7471108
  131.5 12.8 %copy-start.13 = (bf16[4,608,128]{2,1,0:T(8,128)(2,1)}, bf16[4,608,128]{2,1,0:T(8,128)(2,1)S(1)}, u32[]{:S(2)}) copy-start(bf16[4,608,128]{2,1,0:T(8,128)(2,1)S(1)} %collective-permute-done.2) | copy-start | bytes 1867780
  131.5 12.7 %copy-start.14 = (bf16[4,608,128]{2,1,0:T(8,128)(2,1)}, bf16[4,608,128]{2,1,0:T(8,128)(2,1)S(1)}, u32[]{:S(2)}) copy-start(bf16[4,608,128]{2,1,0:T(8,128)(2,1)S(1)} %collective-permute-done.3) | copy-start | bytes 1867780
  154.4 105.0 %reduce-scatter.6.cloned.1.call-start = ((), (), s32[]{:S(2)}) async-start(), calls=%async_computation.5 | async-start | bytes 2621440 | tf_op jit(solution)/shard_map/reduce_scatter | solution.py:237
  154.6 7.0 %copy-start.16 = (bf16[4,608,128]{2,1,0:T(8,128)(2,1)S(1)}, bf16[4,608,128]{2,1,0:T(8,128)(2,1)}, u32[]{:S(2)}) copy-start(bf16[4,608,128]{2,1,0:T(8,128)(2,1)} %copy-done.15) | copy-start | bytes 1867780
  156.4 7.4 %copy-start.29 = (bf16[1024,1024]{1,0:T(8,128)(2,1)S(1)}, bf16[1024,1024]{1,0:T(8,128)(2,1)}, u32[]{:S(2)}) copy-start(bf16[1024,1024]{1,0:T(8,128)(2,1)} %copy-done.28) | copy-start | bytes 6291460
  162.3 1.8 copy-start.31
  162.3 1.9 copy-start.33
  168.0 2.3 slice-start.2
  168.0 2.3 slice-start.3
  168.0 2.3 slice-start.4
  173.6 23.6 %collective-permute-start.11 = (bf16[160,1280]{1,0:T(8,128)(2,1)}, bf16[160,1280]{1,0:T(8,128)(2,1)}, u32[]{:S(2)}, u32[]{:S(2)}) collective-permute-start(bf16[160,1280]{1,0:T(8,128)(2,1)} %get-tuple-element.62), channel_id=1, source_target_pairs={{0,24},{2,26},{4,28},{6,30},{8,0},{10,2},{12,4},{14,6},{16,8},{18,... | collective-permute-start | bytes 1228808 | tf_op jit(solution)/shard_map/ppermute | solution.py:253
  176.5 67.1 %collective-permute-start.10 = (bf16[160,1280]{1,0:T(8,128)(2,1)}, bf16[160,1280]{1,0:T(8,128)(2,1)}, u32[]{:S(2)}, u32[]{:S(2)}) collective-permute-start(bf16[160,1280]{1,0:T(8,128)(2,1)} %get-tuple-element.63), channel_id=1, source_target_pairs={{0,16},{2,18},{4,20},{6,22},{8,24},{10,26},{12,28},{14,30},{16,0},... | collective-permute-start | bytes 1228808 | tf_op jit(solution)/shard_map/ppermute | solution.py:253
  176.5 67.1 %collective-permute-start.9 = (bf16[160,1280]{1,0:T(8,128)(2,1)}, bf16[160,1280]{1,0:T(8,128)(2,1)}, u32[]{:S(2)}, u32[]{:S(2)}) collective-permute-start(bf16[160,1280]{1,0:T(8,128)(2,1)} %get-tuple-element.61), channel_id=1, source_target_pairs={{0,8},{2,10},{4,12},{6,14},{8,16},{10,18},{12,20},{14,22},{16,24},... | collective-permute-start | bytes 1228808 | tf_op jit(solution)/shard_map/ppermute | solution.py:253
  194.6 51.5 %collective-permute-start.6 = (bf16[25,256,16]{1,2,0:T(8,128)(2,1)}, bf16[25,256,16]{1,2,0:T(8,128)(2,1)S(1)}, u32[]{:S(2)}, u32[]{:S(2)}) collective-permute-start(bf16[25,256,16]{1,2,0:T(8,128)(2,1)} %copy.87), channel_id=1, source_target_pairs={{2,0},{4,2},{6,4},{8,6},{10,8},{12,10},{14,12},{16,14},{18,16},{20... | collective-permute-start | bytes 614408 | tf_op jit(solution)/shard_map/ppermute | solution.py:152
  197.2 48.9 %copy-start.6 = (f32[25,256,128]{2,1,0:T(8,128)S(1)}, f32[25,256,128]{2,1,0:T(8,128)}, u32[]{:S(2)}) copy-start(f32[25,256,128]{2,1,0:T(8,128)} %get-tuple-element.17) | copy-start | bytes 9830404
  197.3 48.9 %copy-start.27 = (f32[25,256]{1,0:T(8,128)S(1)}, f32[25,256]{1,0:T(8,128)}, u32[]{:S(2)}) copy-start(f32[25,256]{1,0:T(8,128)} %copy-done.26) | copy-start | bytes 76804
  197.3 48.9 %collective-permute-start.5 = (bf16[25,256,16]{1,2,0:T(8,128)(2,1)}, bf16[25,256,16]{1,2,0:T(8,128)(2,1)S(1)}, u32[]{:S(2)}, u32[]{:S(2)}) collective-permute-start(bf16[25,256,16]{1,2,0:T(8,128)(2,1)} %copy.86), channel_id=1, source_target_pairs={{0,2},{2,4},{4,6},{6,8},{8,10},{10,12},{12,14},{14,16},{16,18},{18... | collective-permute-start | bytes 614408 | tf_op jit(solution)/shard_map/ppermute | solution.py:151
  (11 other events, 11.5 us)
Sparse Core Ops, SparseCore 0:
  42.8 38.3 all-gather.1
  83.4 36.2 reduce-scatter.3
  154.5 35.7 reduce-scatter.7
  192.4 63.0 reduce-scatter.5

commit v2 on v1

--- a/solution.py
+++ b/solution.py
@@ -153,6 +153,17 @@
     return jnp.concatenate([low, high], axis=2)
 
 
+def all_channels(own):
+    shares = lax.axis_size("chan")
+    if shares != 2:
+        return lax.all_gather(own, "chan", axis=1, tiled=True)
+    other = lax.ppermute(own, "chan", [(0, 1), (1, 0)])
+    place = lax.axis_index("chan")
+    low = jnp.where(place == 0, own, other)
+    high = jnp.where(place == 0, other, own)
+    return jnp.concatenate([low, high], axis=1)
+
+
 def hot_rows(size, codes):
     return (jnp.arange(size, dtype=jnp.int32)[:, None] == codes[None, :]).astype(jnp.bfloat16)
 
@@ -225,7 +236,7 @@
     return frames, widths
 
 
-def weight_grads(frames, widths, grads_all, local):
+def weight_grads(frames, widths, grads_all, local, first_done):
     count = lax.axis_size("graph")
     near = 4
     far = count // near
@@ -243,7 +254,7 @@
         ).astype(jnp.float32)
 
     def settle_direct(partial):
-        partial = partial.astype(jnp.bfloat16)
+        partial, _ = lax.optimization_barrier((partial.astype(jnp.bfloat16), first_done))
         place = lax.axis_index("graph") // near
         total = lax.dynamic_index_in_dim(partial, place, axis=0, keepdims=False)
         total = total.astype(jnp.float32)
@@ -323,7 +334,7 @@
     picks = hot_rows(atoms + 2 * halo, edge_source)
     own = to_frames([(normed, picks[:atoms]), (table_end, picks[atoms:])], rotations, ones)
     own, grads = lax.optimization_barrier((own, grads))
-    piece = lax.all_gather(own, "chan", axis=1, tiled=True)
+    piece = all_channels(own)
 
     grads_side = swap(grads, 2)
     pair = swap(jnp.stack([grads, grads_side]), 1)
@@ -355,7 +366,7 @@
         scaled
         - values * (inverse**2 * tally / (25 * channels))[None, None, :]
     ).astype(jnp.bfloat16)
-    grad_zero, grad_one, grad_two = weight_grads(frames, widths, grads_all, local)
+    grad_zero, grad_one, grad_two = weight_grads(frames, widths, grads_all, local, incoming)
     return (update, grad_embed, grad_zero, grad_one, grad_two)
 
 

time: 270 us -> 258 us (0.956)
  the two profiles are of different devices: /device:TPU:4 before, /device:TPU:0 now
where the time goes in v2:
time: 258 us; the launch traced here: 257 us
  local copies, waits for them, and re-layouts  82.5 us (32%)
  waiting for transfers between devices  41.2 us (16%)
  matrix products  38.5 us (15%)
  other arithmetic  26.3 us (10%)
  starting transfers between devices  23.9 us (9%)
  Pallas kernels  19.2 us (7%)
  between operations  14.4 us (6%)
  blocking collectives  10.8 us (4%)
    ppermute x3, waiting for transfers between devices, settle_direct(): total = total + lax.ppermute(chunk, 'graph', shift).astype(jnp.float32)  34.1 us
    unnamed x97, local copies, waits for them, and re-layouts  23.3 us
    dot_general x3, matrix products, across(): lax.dot_general(left, right, (((0,), (0,)), ((), ())), preferred_element_...  13.7 us
    dot_general x5, matrix products, product(): return jnp.dot(left, right, preferred_element_type=jnp.float32)  13.7 us
    ppermute x3, starting transfers between devices, settle_direct(): total = total + lax.ppermute(chunk, 'graph', shift).astype(jnp.float32)  11.7 us
    dot_general x3, matrix products, contract(): lax.dot_general(left, right, (((2,), (1,)), ((), ())), preferred_element_...  10.1 us
    pallas_call x2, Pallas kernels, to_atoms(): pl.pallas_call(functools.partial(atoms_kernel, count), grid=(local // blo...  9.95 us
    pallas_call x2, Pallas kernels, to_frames(): pl.pallas_call(frames_kernel, grid=(local // block,), in_specs=specs, out...  9.25 us
  transfers between devices with their start and end apart: 16, of which 6 were waited for; matrix products, arithmetic and copies ran while one was open for 48% of the time, Pallas kernels for 6%

profile of v2, /device:TPU:0, one launch (start us, length us, event | category | flops | bytes accessed | tf_op | source)
XLA Modules:
  0.0 256.8 jit_solution(17105075791098122900)
XLA Ops:
  8.1 2.3 fusion.2
  10.4 5.9 %psum.14 = f32[128]{0:T(128)S(1)} all-reduce(f32[128]{0:T(128)S(1)} %fusion.2), channel_id=1, replica_groups=mesh['graph'=16,'chan'=2] {'chan'}, use_global_device_ids=true, to_apply=%region_1.0 | all-reduce | flops 128 | bytes 1024 | tf_op jit(solution)/shard_map/psum | solution.py:326
  19.0 2.0 reshape.209
  22.2 3.4 %collective-permute-start.1 = (bf16[25,256,16]{1,2,0:T(8,128)(2,1)S(1)}, bf16[25,256,16]{1,2,0:T(8,128)(2,1)}, u32[]{:S(2)}, u32[]{:S(2)}) collective-permute-start(bf16[25,256,16]{1,2,0:T(8,128)(2,1)S(1)} %copy.69), channel_id=1, source_target_pairs={{2,0},{4,2},{6,4},{8,6},{10,8},{12,10},{14,12},{16,14},{18,16},{20... | collective-permute-start | bytes 614408 | tf_op jit(solution)/shard_map/ppermute | solution.py:152
  30.2 4.5 %shard_map.156 = bf16[19,256,128]{2,1,0:T(8,128)(2,1)} custom-call(bf16[25,256,128]{2,1,0:T(8,128)(2,1)} %refs_0_.1, bf16[128,128]{1,0:T(8,128)(2,1)} %get-tuple-element.122.refs_1_, f32[475,128]{1,0:T(8,128)} %convolution_bitcast_fusion.4.refs_4_.refs_2_.rotations, f32[1,128]{1,0:T(1,128)} %bitcast.223), custom_call_target="tpu_custom_call" | custom-call | tf_op jit(solution)/shard_map/pallas_call | solution.py:88
  35.7 1.6 copy.71.refs_2_
  37.8 4.8 %shard_map.155 = bf16[19,256,128]{2,1,0:T(8,128)(2,1)} custom-call(bf16[25,256,128]{2,1,0:T(8,128)(2,1)} %copy-done.3, bf16[128,128]{1,0:T(8,128)(2,1)} %slice.316.refs_1_, bf16[25,256,32]{2,1,0:T(8,128)(2,1)} %copy.71.refs_2_, bf16[32,128]{1,0:T(8,128)(2,1)} %slice.319.refs_3_, f32[475,128]{1,0:T(8,128)} %convolution_bitcast_fusion.4.refs_4_.refs_2_.rotations, ...), custom_call_target="tpu_custom_call" | custom-call | tf_op jit(solution)/shard_map/pallas_call | solution.py:88
  42.6 1.8 fusion.100
  44.4 1.7 fusion.99
  46.1 1.5 collective-permute-start.2
  47.6 4.0 %fusion.1 = bf16[2560,128]{0,1:T(8,128)(2,1)S(1)} fusion(bf16[19,256,128]{2,1,0:T(8,128)(2,1)} %shard_map.156, bf16[5,256,2560]{2,1,0:T(8,128)(2,1)} %param.14), kind=kOutput, calls=%fused_computation.7 | convolution fusion | flops 839188480 | bytes 8454144 | tf_op jit(solution)/shard_map/dot_general | solution.py:49
  53.0 5.9 %fusion.8 = bf16[2048,256]{0,1:T(8,128)(2,1)S(1)} fusion(bf16[2048,2048]{1,0:T(8,128)(2,1)} %bitcast.225, bf16[1024,128]{1,0:T(8,128)(2,1)S(1)} %bitcast_negate_fusion.1, bf16[1024,128]{1,0:T(8,128)(2,1)} %bitcast.195, bf16[1024,128]{1,0:T(8,128)(2,1)S(1)} %bitcast.177), kind=kOutput, calls=%fused_computation.29 | convolution fusion | flops 2152202240 | bytes 10223616 | tf_op jit(solution)/shard_map/dot_general | solution.py:49
  61.2 3.7 %fusion.9 = bf16[1536,256]{0,1:T(8,128)(2,1)S(1)} fusion(bf16[1536,1536]{1,0:T(8,128)(2,1)} %bitcast.229, bf16[768,128]{1,0:T(8,128)(2,1)S(1)} %bitcast_negate_fusion, bf16[768,128]{1,0:T(8,128)(2,1)S(1)} %bitcast.208, bf16[768,128]{1,0:T(8,128)(2,1)S(1)} %bitcast.185), kind=kOutput, calls=%fused_computation.30 | convolution fusion | flops 1211498496 | bytes 6094848 | tf_op jit(solution)/shard_map/dot_general | solution.py:49
  75.7 1.8 broadcast_select_fusion
  79.4 2.6 %convolution_bitcast_fusion.1 = f32[1536,256]{0,1:T(8,128)} fusion(bf16[1536,1536]{1,0:T(8,128)(2,1)S(1)} %bitcast.232, bf16[1536,128]{1,0:T(8,128)(2,1)S(1)} %bitcast.187, bf16[1536,128]{1,0:T(8,128)(2,1)S(1)} %bitcast.189), kind=kOutput, calls=%fused_computation.24 | convolution fusion | flops 1209532416 | bytes 7077888 | tf_op jit(solution)/shard_map/dot_general | solution.py:45
  82.0 3.0 %copy.74 = f32[1536,256]{1,0:T(8,128)} copy(f32[1536,256]{0,1:T(8,128)} %convolution_bitcast_fusion.1) | data formatting | bytes 3145728 | tf_op jit(solution)/shard_map/dot_general | solution.py:45
  88.8 1.7 collective-permute-start.3
  90.9 3.5 %pad_maximum_fusion = bf16[2,19,256,128]{3,2,1,0:T(8,128)(2,1)} fusion(bf16[1,19,256,128]{3,2,1,0:T(8,128)(2,1)} %bitcast.57, bf16[1,19,256,128]{3,2,1,0:T(8,128)(2,1)} %bitcast.56), kind=kLoop, calls=%fused_computation.28 | loop fusion | flops 1245184 | bytes 4980736 | tf_op jit(solution)/shard_map/stack | solution.py:340
  94.5 3.1 %convolution_bitcast_fusion.3 = f32[1280,128]{0,1:T(8,128)} fusion(bf16[2560,128]{1,0:T(8,128)(2,1)S(1)} %bitcast.172, bf16[1280,2560]{1,0:T(8,128)(2,1)S(1)} %bitcast.165), kind=kOutput, calls=%fused_computation.31 | convolution fusion | flops 838860800 | bytes 7864320 | tf_op jit(solution)/shard_map/dot_general | solution.py:45
  97.6 3.7 %convolution_bitcast_fusion.2 = f32[2048,256]{0,1:T(8,128)} fusion(bf16[2048,2048]{1,0:T(8,128)(2,1)S(1)} %bitcast.228, bf16[2048,128]{1,0:T(8,128)(2,1)S(1)} %bitcast.182, bf16[2048,128]{1,0:T(8,128)(2,1)S(1)} %bitcast.180), kind=kOutput, calls=%fused_computation.25 | convolution fusion | flops 2149580800 | bytes 11534336 | tf_op jit(solution)/shard_map/dot_general | solution.py:45
  101.4 1.8 fusion.98
  103.9 1.7 fusion.97
  107.7 3.0 %copy.73 = f32[2048,256]{1,0:T(8,128)} copy(f32[2048,256]{0,1:T(8,128)} %convolution_bitcast_fusion.2) | data formatting | bytes 4194304 | tf_op jit(solution)/shard_map/dot_general | solution.py:45
  114.2 2.0 collective-permute-done.5
  126.9 3.8 %fusion.25 = bf16[4,192,768]{2,1,0:T(8,128)(2,1)} fusion(bf16[768,1024]{1,0:T(8,128)(2,1)} %constant_dynamic-update-slice_fusion.48, bf16[4,96,1024]{2,1,0:T(8,128)(2,1)S(1)} %get-tuple-element.83, bf16[4,96,1024]{2,1,0:T(8,128)(2,1)S(1)} %get-tuple-element.82), kind=kOutput, calls=%fused_computation.43 | convolution fusion | flops 1211695104 | bytes 4325376 | tf_op jit(solution)/shard_map/dot_general | solution.py:55
  131.8 1.8 constant_dynamic-update-slice_fusion.11
  133.6 1.7 constant_dynamic-update-slice_fusion.10
  135.3 1.7 constant_dynamic-update-slice_fusion.9
  137.0 1.7 constant_dynamic-update-slice_fusion.8
  140.6 3.7 %fusion.15 = bf16[4,256,1024]{2,1,0:T(8,128)(2,1)} fusion(bf16[1024,1024]{1,0:T(8,128)(2,1)S(1)} %constant_dynamic-update-slice_fusion.24, bf16[4,128,1024]{2,1,0:T(8,128)(2,1)S(1)} %copy-done.22, bf16[4,128,1024]{2,1,0:T(8,128)(2,1)S(1)} %copy-done.20), kind=kOutput, calls=%fused_computation.37 | convolution fusion | flops 2152726528 | bytes 6291456 | tf_op jit(solution)/shard_map/dot_general | solution.py:55
  145.7 1.8 slice.268
  147.5 1.7 slice.342
  149.2 1.6 slice.284
  150.8 1.6 slice.283
  153.1 4.8 %shard_map.157 = bf16[25,256,128]{2,1,0:T(8,128)(2,1)} custom-call(f32[19,256,128]{2,1,0:T(8,128)} %copy-done.6, f32[475,128]{1,0:T(8,128)} %convolution_bitcast_fusion.4.refs_4_.refs_2_.rotations, f32[1,128]{1,0:T(1,128)} %bitcast.224, bf16[128,128]{1,0:T(8,128)(2,1)} %get-tuple-element.121.refs_0_), custom_call_target="tpu_custom_call" | custom-call | tf_op jit(solution)/shard_map/pallas_call | solution.py:121
  157.9 2.0 fusion.95
  159.8 5.2 %shard_map.158 = (f32[25,256,128]{2,1,0:T(8,128)}, bf16[25,256,32]{2,1,0:T(8,128)(2,1)}) custom-call(bf16[19,256,128]{2,1,0:T(8,128)(2,1)} %bitcast.193, f32[475,128]{1,0:T(8,128)} %convolution_bitcast_fusion.4.refs_4_.refs_2_.rotations, f32[1,128]{1,0:T(1,128)} %broadcast_in_dim.28.refs_5_.scale, bf16[128,128]{1,0:T(8,128)(2,1)} %slice.340.refs_0_, ...), custom_call_target="tpu_custom_call" | custom-call | tf_op jit(solution)/shard_map/pallas_call | solution.py:121
  165.0 3.8 %fusion.96 = (bf16[25,256,16]{2,1,0:T(8,128)(2,1)S(1)}, bf16[25,256,16]{2,1,0:T(8,128)(2,1)}) fusion(bf16[25,256,32]{2,1,0:T(8,128)(2,1)} %get-tuple-element.19), kind=kLoop, calls=%fused_computation.202 | loop fusion | bytes 819200 | tf_op jit(solution)/shard_map/slice | solution.py:152
  168.8 2.6 %copy.86 = bf16[25,256,16]{1,2,0:T(8,128)(2,1)} copy(bf16[25,256,16]{2,1,0:T(8,128)(2,1)} %get-tuple-element.69) | data formatting | bytes 409600 | tf_op jit(solution)/shard_map/slice | solution.py:151
  173.9 3.4 %collective-permute-start.7 = (bf16[25,256,16]{1,2,0:T(8,128)(2,1)}, bf16[25,256,16]{1,2,0:T(8,128)(2,1)S(1)}, u32[]{:S(2)}, u32[]{:S(2)}) collective-permute-start(bf16[25,256,16]{1,2,0:T(8,128)(2,1)} %copy.87), channel_id=1, source_target_pairs={{2,0},{4,2},{6,4},{8,6},{10,8},{12,10},{14,12},{16,14},{18,16},{20... | collective-permute-start | bytes 614408 | tf_op jit(solution)/shard_map/ppermute | solution.py:152
  177.3 2.5 convolution_convert_fusion.1
  179.8 4.5 %collective-permute-done.6 = bf16[25,256,16]{1,2,0:T(8,128)(2,1)} collective-permute-done((bf16[25,256,16]{1,2,0:T(8,128)(2,1)}, bf16[25,256,16]{1,2,0:T(8,128)(2,1)}, u32[]{:S(2)}, u32[]{:S(2)}) %collective-permute-start.6) | collective-permute-done | bytes 204832 | tf_op jit(solution)/shard_map/ppermute | solution.py:151
  186.4 11.1 %collective-permute-start.12 = (bf16[160,1280]{1,0:T(8,128)(2,1)}, bf16[160,1280]{1,0:T(8,128)(2,1)}, u32[]{:S(2)}, u32[]{:S(2)}) collective-permute-start(bf16[160,1280]{1,0:T(8,128)(2,1)} %get-tuple-element.66), channel_id=1, source_target_pairs={{0,24},{2,26},{4,28},{6,30},{8,0},{10,2},{12,4},{14,6},{16,8},{18,... | collective-permute-start | bytes 1228808 | tf_op jit(solution)/shard_map/ppermute | solution.py:264
  198.1 2.8 %fusion.5 = (f32[128]{0:T(128)S(1)}, f32[25,256,128]{2,1,0:T(8,128)}) fusion(bf16[25,256,128]{2,1,0:T(8,128)(2,1)S(1)} %copy-done, f32[25,256,128]{2,1,0:T(8,128)S(1)} %copy-done.7, bf16[25,256,32]{1,2,0:T(8,128)(2,1)S(1)} %constant_dynamic-update-slice_fusion.6, s32[32]{0:T(128)S(1)} %copy-done.24, f32[25,256]{1,0:T(8,128)S(1)} %copy-done.17, ...), kind=kOutput, calls=%fused_computation.19 | convolution fusion | flops 57347968 | bytes 8628352 | tf_op jit(solution)/shard_map/dot_general | solution.py:45
  200.9 4.9 %psum.15 = f32[128]{0:T(128)S(1)} all-reduce(f32[128]{0:T(128)S(1)} %get-tuple-element.123), channel_id=1, replica_groups=mesh['graph'=16,'chan'=2] {'chan'}, use_global_device_ids=true, to_apply=%region_4.5 | all-reduce | flops 128 | bytes 1024 | tf_op jit(solution)/shard_map/psum | solution.py:364
  205.8 3.6 %fusion.7 = bf16[25,256,128]{2,1,0:T(8,128)(2,1)} fusion(f32[25,256,128]{2,1,0:T(8,128)} %get-tuple-element.124, bf16[25,256,128]{2,1,0:T(8,128)(2,1)S(1)} %copy-done, f32[128]{0:T(128)S(1)} %multiply_multiply_fusion), kind=kLoop, calls=%fused_computation.21 | loop fusion | flops 3276800 | bytes 6554112 | tf_op jit(solution)/shard_map/convert_element_type | solution.py:368
  209.5 7.0 %collective-permute-done.12 = bf16[160,1280]{1,0:T(8,128)(2,1)} collective-permute-done((bf16[160,1280]{1,0:T(8,128)(2,1)}, bf16[160,1280]{1,0:T(8,128)(2,1)}, u32[]{:S(2)}, u32[]{:S(2)}) %collective-permute-start.12) | collective-permute-done | bytes 409632 | tf_op jit(solution)/shard_map/ppermute | solution.py:264
  216.5 27.0 %collective-permute-done.11 = bf16[160,1280]{1,0:T(8,128)(2,1)} collective-permute-done((bf16[160,1280]{1,0:T(8,128)(2,1)}, bf16[160,1280]{1,0:T(8,128)(2,1)}, u32[]{:S(2)}, u32[]{:S(2)}) %collective-permute-start.11) | collective-permute-done | bytes 409632 | tf_op jit(solution)/shard_map/ppermute | solution.py:264
  (192 shorter events, 65.0 us)
Async XLA Ops:
  7.2 9.3 %copy-start = (bf16[25,256,128]{2,1,0:T(8,128)(2,1)S(1)}, bf16[25,256,128]{2,1,0:T(8,128)(2,1)}, u32[]{:S(2)}) copy-start(bf16[25,256,128]{2,1,0:T(8,128)(2,1)} %param.12) | copy-start | bytes 4915204
  7.2 152.6 %reduce-scatter.4.cloned.1.call-start = ((), (), s32[]{:S(2)}) async-start(), calls=%async_computation.3 | async-start | bytes 3735552 | tf_op jit(solution)/shard_map/reduce_scatter | solution.py:343
  10.4 7.1 %copy-start.24 = (s32[32]{0:T(128)S(1)}, s32[32]{0:T(128)}, u32[]{:S(2)}) copy-start(s32[32]{0:T(128)} %param.18) | copy-start | bytes 388
  16.4 2.5 copy-start.16
  17.5 4.7 %copy-start.3 = (bf16[25,256,128]{2,1,0:T(8,128)(2,1)}, bf16[25,256,128]{2,1,0:T(8,128)(2,1)S(1)}, u32[]{:S(2)}) copy-start(bf16[25,256,128]{2,1,0:T(8,128)(2,1)S(1)} %fusion.4.refs_0_) | copy-start | bytes 4915204
  17.5 8.3 %copy-start.25 = (s32[128]{0:T(128)S(1)}, s32[128]{0:T(128)}, u32[]{:S(2)}) copy-start(s32[128]{0:T(128)} %param.19) | copy-start | bytes 1540
  21.0 7.4 %copy-start.26 = (s32[128]{0:T(128)S(1)}, s32[128]{0:T(128)}, u32[]{:S(2)}) copy-start(s32[128]{0:T(128)} %param.21) | copy-start | bytes 1540
  22.0 7.5 %copy-start.23 = (s32[128]{0:T(128)S(1)}, s32[128]{0:T(128)}, u32[]{:S(2)}) copy-start(s32[128]{0:T(128)} %param.20) | copy-start | bytes 1540
  22.2 12.5 %collective-permute-start.1 = (bf16[25,256,16]{1,2,0:T(8,128)(2,1)S(1)}, bf16[25,256,16]{1,2,0:T(8,128)(2,1)}, u32[]{:S(2)}, u32[]{:S(2)}) collective-permute-start(bf16[25,256,16]{1,2,0:T(8,128)(2,1)S(1)} %copy.69), channel_id=1, source_target_pairs={{2,0},{4,2},{6,4},{8,6},{10,8},{12,10},{14,12},{16,14},{18,16},{20... | collective-permute-start | bytes 614408 | tf_op jit(solution)/shard_map/ppermute | solution.py:152
  25.8 8.9 %collective-permute-start = (bf16[25,256,16]{1,2,0:T(8,128)(2,1)S(1)}, bf16[25,256,16]{1,2,0:T(8,128)(2,1)S(1)}, u32[]{:S(2)}, u32[]{:S(2)}) collective-permute-start(bf16[25,256,16]{1,2,0:T(8,128)(2,1)S(1)} %copy.68), channel_id=1, source_target_pairs={{0,2},{2,4},{4,6},{6,8},{8,10},{10,12},{12,14},{14,16},{16,18},{18... | collective-permute-start | bytes 614408 | tf_op jit(solution)/shard_map/ppermute | solution.py:151
  46.1 44.9 %collective-permute-start.8 = (bf16[19,256,128]{2,1,0:T(8,128)(2,1)}, bf16[19,256,128]{2,1,0:T(8,128)(2,1)}, u32[]{:S(2)}, u32[]{:S(2)}) collective-permute-start(bf16[19,256,128]{2,1,0:T(8,128)(2,1)} %shard_map.156), channel_id=1, source_target_pairs={{0,4},{2,6},{4,0},{6,2},{8,12},{10,14},{12,8},{14,10},{16,20},{18,... | collective-permute-start | bytes 3735560 | tf_op jit(solution)/shard_map/ppermute | solution.py:144
  46.1 29.6 %collective-permute-start.2 = (bf16[19,256,128]{2,1,0:T(8,128)(2,1)}, bf16[19,256,128]{2,1,0:T(8,128)(2,1)}, u32[]{:S(2)}, u32[]{:S(2)}) collective-permute-start(bf16[19,256,128]{2,1,0:T(8,128)(2,1)} %shard_map.155), channel_id=1, source_target_pairs={{0,1},{1,0},{2,3},{3,2},{4,5},{5,4},{6,7},{7,6},{8,9},{9,8},{10,11... | collective-permute-start | bytes 3735560 | tf_op jit(solution)/shard_map/ppermute | solution.py:160
  58.9 2.3 copy-start.13
  70.3 2.7 %copy-start.14 = (bf16[3,256,128]{2,1,0:T(8,128)(2,1)S(1)}, bf16[3,256,128]{2,1,0:T(8,128)(2,1)}, u32[]{:S(2)}) copy-start(bf16[3,256,128]{2,1,0:T(8,128)(2,1)} %get-tuple-element.74) | copy-start | bytes 589828
  72.0 2.5 copy-start.11
  72.1 173.9 %reduce-scatter.8.cloned.1.call-start = ((), (), s32[]{:S(2)}) async-start(), calls=%async_computation.5 | async-start | bytes 1474560 | tf_op jit(solution)/shard_map/reduce_scatter | solution.py:248
  73.8 5.6 %slice-start.5 = ((s8[4718592]{0:T(1024)(128)(4,1)}), s8[4194304]{0:T(1024)(128)(4,1)S(1)}, s32[]{:S(2)}) async-start(s8[4718592]{0:T(1024)(128)(4,1)} %bitcast.230), calls=%async_computation.11 | async-start | bytes 8388608
  75.3 4.1 %slice-start.6 = ((s8[4718592]{0:T(1024)(128)(4,1)}), s8[524288]{0:T(1024)(128)(4,1)S(1)}, s32[]{:S(2)}) async-start(s8[4718592]{0:T(1024)(128)(4,1)} %bitcast.230), calls=%async_computation.12 | async-start | bytes 1048576
  77.5 1.0 copy-start.1
  85.0 1.4 copy-start.2
  86.4 1.0 copy-start.10
  86.4 11.3 %slice-start.3 = ((s8[8388608]{0:T(1024)(128)(4,1)}), s8[4194304]{0:T(1024)(128)(4,1)S(1)}, s32[]{:S(2)}) async-start(s8[8388608]{0:T(1024)(128)(4,1)} %bitcast.226), calls=%async_computation.9 | async-start | bytes 8388608
  86.4 8.1 %slice-start = ((s8[6553600]{0:T(1024)(128)(4,1)}), s8[4194304]{0:T(1024)(128)(4,1)S(1)}, s32[]{:S(2)}) async-start(s8[6553600]{0:T(1024)(128)(4,1)} %bitcast.163), calls=%async_computation.6 | async-start | bytes 8388608
  87.5 7.1 %slice-start.1 = ((s8[6553600]{0:T(1024)(128)(4,1)}), s8[2359296]{0:T(1024)(128)(4,1)S(1)}, s32[]{:S(2)}) async-start(s8[6553600]{0:T(1024)(128)(4,1)} %bitcast.163), calls=%async_computation.7 | async-start | bytes 4718592
  88.8 25.4 %collective-permute-start.3 = (bf16[4,608,128]{2,1,0:T(8,128)(2,1)}, bf16[4,608,128]{2,1,0:T(8,128)(2,1)S(1)}, u32[]{:S(2)}, u32[]{:S(2)}) collective-permute-start(bf16[4,608,128]{2,1,0:T(8,128)(2,1)} %get-tuple-element.57), channel_id=1, source_target_pairs={{0,4},{2,6},{4,0},{6,2},{8,12},{10,14},{12,8},{14,10},{16,20},{18,... | collective-permute-start | bytes 1867784 | tf_op jit(solution)/shard_map/ppermute | solution.py:144
  90.5 23.8 %collective-permute-start.4 = (bf16[4,608,128]{2,1,0:T(8,128)(2,1)}, bf16[4,608,128]{2,1,0:T(8,128)(2,1)}, u32[]{:S(2)}, u32[]{:S(2)}) collective-permute-start(bf16[4,608,128]{2,1,0:T(8,128)(2,1)} %get-tuple-element.56), channel_id=1, source_target_pairs={{0,2},{2,0},{4,6},{6,4},{8,10},{10,8},{12,14},{14,12},{16,18},{18,... | collective-permute-start | bytes 1867784 | tf_op jit(solution)/shard_map/ppermute | solution.py:144
  90.5 25.7 %collective-permute-start.5 = (bf16[4,608,128]{2,1,0:T(8,128)(2,1)}, bf16[4,608,128]{2,1,0:T(8,128)(2,1)}, u32[]{:S(2)}, u32[]{:S(2)}) collective-permute-start(bf16[4,608,128]{2,1,0:T(8,128)(2,1)} %get-tuple-element.55), channel_id=1, source_target_pairs={{0,6},{2,4},{4,2},{6,0},{8,14},{10,12},{12,10},{14,8},{16,22},{18,... | collective-permute-start | bytes 1867784 | tf_op jit(solution)/shard_map/ppermute | solution.py:144
  90.9 6.7 %slice-start.4 = ((s8[8388608]{0:T(1024)(128)(4,1)}), s8[4194304]{0:T(1024)(128)(4,1)S(1)}, s32[]{:S(2)}) async-start(s8[8388608]{0:T(1024)(128)(4,1)} %bitcast.226), calls=%async_computation.10 | async-start | bytes 8388608
  94.5 28.3 %collective-permute-start.9 = (bf16[2,19,256,128]{3,2,1,0:T(8,128)(2,1)}, bf16[2,19,256,128]{3,2,1,0:T(8,128)(2,1)}, u32[]{:S(2)}, u32[]{:S(2)}) collective-permute-start(bf16[2,19,256,128]{3,2,1,0:T(8,128)(2,1)} %pad_maximum_fusion), channel_id=1, source_target_pairs={{0,2},{2,0},{4,6},{6,4},{8,10},{10,8},{12,14},{14,12},{16,18},{18,... | collective-permute-start | bytes 7471112 | tf_op jit(solution)/shard_map/ppermute | solution.py:144
  110.7 1.9 copy-start.4
  110.7 2.0 copy-start.15
  110.7 2.6 %copy-start.12 = (bf16[4,256,128]{2,1,0:T(8,128)(2,1)S(1)}, bf16[4,256,128]{2,1,0:T(8,128)(2,1)}, u32[]{:S(2)}) copy-start(bf16[4,256,128]{2,1,0:T(8,128)(2,1)} %get-tuple-element.72) | copy-start | bytes 786436
  110.8 3.3 %copy-start.5 = (f32[1536,256]{1,0:T(8,128)S(1)}, f32[1536,256]{1,0:T(8,128)}, u32[]{:S(2)}) copy-start(f32[1536,256]{1,0:T(8,128)} %copy.74) | copy-start | bytes 4718596
  114.2 6.5 %copy-start.6 = (f32[19,256,128]{2,1,0:T(8,128)}, f32[19,256,128]{2,1,0:T(8,128)S(1)}, u32[]{:S(2)}) copy-start(f32[19,256,128]{2,1,0:T(8,128)S(1)} %fusion.74.values) | copy-start | bytes 7471108
  114.2 38.2 %copy-start.8 = (bf16[4,608,128]{2,1,0:T(8,128)(2,1)}, bf16[4,608,128]{2,1,0:T(8,128)(2,1)S(1)}, u32[]{:S(2)}) copy-start(bf16[4,608,128]{2,1,0:T(8,128)(2,1)S(1)} %collective-permute-done.3) | copy-start | bytes 1867780
  120.8 1.0 copy-start.19
  130.8 117.0 %reduce-scatter.6.cloned.1.call-start = ((), (), s32[]{:S(2)}) async-start(), calls=%async_computation.4 | async-start | bytes 2621440 | tf_op jit(solution)/shard_map/reduce_scatter | solution.py:248
  131.8 8.3 %copy-start.18 = (bf16[1024,1024]{1,0:T(8,128)(2,1)S(1)}, bf16[1024,1024]{1,0:T(8,128)(2,1)}, u32[]{:S(2)}) copy-start(bf16[1024,1024]{1,0:T(8,128)(2,1)} %constant_dynamic-update-slice_fusion.28) | copy-start | bytes 6291460
  138.7 1.8 copy-start.20
  138.7 1.9 copy-start.22
  168.8 8.4 %slice-start.2 = ((bf16[4,608,128]{2,1,0:T(8,128)(2,1)}), bf16[4,160,128]{2,1,0:T(8,128)(2,1)S(1)}, s32[]{:S(2)}) async-start(bf16[4,608,128]{2,1,0:T(8,128)(2,1)} %copy-done.8), calls=%async_computation.8 | async-start | bytes 327680 | tf_op jit(solution)/shard_map/slice | solution.py:268
  171.4 12.8 %collective-permute-start.6 = (bf16[25,256,16]{1,2,0:T(8,128)(2,1)}, bf16[25,256,16]{1,2,0:T(8,128)(2,1)}, u32[]{:S(2)}, u32[]{:S(2)}) collective-permute-start(bf16[25,256,16]{1,2,0:T(8,128)(2,1)} %copy.86), channel_id=1, source_target_pairs={{0,2},{2,4},{4,6},{6,8},{8,10},{10,12},{12,14},{14,16},{16,18},{18... | collective-permute-start | bytes 614408 | tf_op jit(solution)/shard_map/ppermute | solution.py:151
  173.9 11.5 %collective-permute-start.7 = (bf16[25,256,16]{1,2,0:T(8,128)(2,1)}, bf16[25,256,16]{1,2,0:T(8,128)(2,1)S(1)}, u32[]{:S(2)}, u32[]{:S(2)}) collective-permute-start(bf16[25,256,16]{1,2,0:T(8,128)(2,1)} %copy.87), channel_id=1, source_target_pairs={{2,0},{4,2},{6,4},{8,6},{10,8},{12,10},{14,12},{16,14},{18,16},{20... | collective-permute-start | bytes 614408 | tf_op jit(solution)/shard_map/ppermute | solution.py:152
  177.3 20.9 %copy-start.17 = (f32[25,256]{1,0:T(8,128)S(1)}, f32[25,256]{1,0:T(8,128)}, u32[]{:S(2)}) copy-start(f32[25,256]{1,0:T(8,128)} %copy-done.16) | copy-start | bytes 76804
  179.8 18.3 %copy-start.7 = (f32[25,256,128]{2,1,0:T(8,128)S(1)}, f32[25,256,128]{2,1,0:T(8,128)}, u32[]{:S(2)}) copy-start(f32[25,256,128]{2,1,0:T(8,128)} %get-tuple-element.18) | copy-start | bytes 9830404
  186.4 30.0 %collective-permute-start.12 = (bf16[160,1280]{1,0:T(8,128)(2,1)}, bf16[160,1280]{1,0:T(8,128)(2,1)}, u32[]{:S(2)}, u32[]{:S(2)}) collective-permute-start(bf16[160,1280]{1,0:T(8,128)(2,1)} %get-tuple-element.66), channel_id=1, source_target_pairs={{0,24},{2,26},{4,28},{6,30},{8,0},{10,2},{12,4},{14,6},{16,8},{18,... | collective-permute-start | bytes 1228808 | tf_op jit(solution)/shard_map/ppermute | solution.py:264
  197.5 46.0 %collective-permute-start.11 = (bf16[160,1280]{1,0:T(8,128)(2,1)}, bf16[160,1280]{1,0:T(8,128)(2,1)}, u32[]{:S(2)}, u32[]{:S(2)}) collective-permute-start(bf16[160,1280]{1,0:T(8,128)(2,1)} %get-tuple-element.67), channel_id=1, source_target_pairs={{0,16},{2,18},{4,20},{6,22},{8,24},{10,26},{12,28},{14,30},{16,0},... | collective-permute-start | bytes 1228808 | tf_op jit(solution)/shard_map/ppermute | solution.py:264
  197.6 46.0 %collective-permute-start.10 = (bf16[160,1280]{1,0:T(8,128)(2,1)}, bf16[160,1280]{1,0:T(8,128)(2,1)}, u32[]{:S(2)}, u32[]{:S(2)}) collective-permute-start(bf16[160,1280]{1,0:T(8,128)(2,1)} %get-tuple-element.65), channel_id=1, source_target_pairs={{0,8},{2,10},{4,12},{6,14},{8,16},{10,18},{12,20},{14,22},{16,24},... | collective-permute-start | bytes 1228808 | tf_op jit(solution)/shard_map/ppermute | solution.py:264
  (2 other events, 1.7 us)
Sparse Core Ops, SparseCore 0:
  72.2 36.4 reduce-scatter.3
  130.9 31.6 reduce-scatter.7
  164.9 60.9 reduce-scatter.5
